TPU v7x, 256 devices: a whole 4x4x8 slice. The times are simulated.
256 devices in a mesh: group: 8 (over z), shard: 32 (over x, y, core).
Axes of the slice: x: 4, y: 4, z: 8, core: 2. Of those that a mesh axis runs over, the one named last changes fastest.
Arguments:
- queries: bfloat16 [1536, 1024], P(('group', 'shard')), may hold values from -12 to 12
- candidates: bfloat16 [1048576, 1024], P(('group', 'shard')), may hold values from -4 to 4
- targets: int32 [1536], replicated, may hold values from 0 to 1048575
Outputs:
- losses: float32 [1536], replicated
- mean_loss: float32 [], replicated
All inputs are finite; a program needn't handle non-finite values.
Results may differ from a plain program's by a relative error of at most 0.0003.
Values may be sent and summed in bfloat16 or wider, within the bound.
No kernel may reach another device: no remote copies, remote signals or barrier semaphores. Data moves between devices by JAX's collectives and lax.ppermute only.
A program may use at most 64 MiB of HBM per device.

v0:
```python
import math

import jax
import jax.numpy as jnp
from jax import lax
from jax.sharding import Mesh
from jax.sharding import PartitionSpec as P

SHARD = ("shard_0", "shard_1", "shard_2")
GROUP_SHARD = ("group", "shard_0", "shard_1", "shard_2")


def laid_out(tiles, dim):
    shape = list(tiles.shape[1:])
    shape[dim] *= tiles.shape[0]
    return jnp.moveaxis(tiles, 0, dim).reshape(shape)


def gather_in_order(value, axes, order):
    tiles = value[None]
    for k in order:
        tiles = lax.all_gather(tiles, axes[k], axis=0, tiled=True)
    held = [lax.axis_size(axes[k]) for k in reversed(order)]
    tiles = tiles.reshape(*held, *value.shape)
    turned = sorted(range(len(order)), key=lambda place: order[len(order) - 1 - place])
    return tiles.transpose(*turned, *range(len(order), tiles.ndim)).reshape(-1, *value.shape)


def gather_axes(value, axes, order, dim):
    return laid_out(gather_in_order(value, axes, order), dim)


def from_everyone(value, axis):
    copies = jnp.broadcast_to(value, (lax.axis_size(axis), *value.shape))
    return lax.all_to_all(copies, axis, split_axis=0, concat_axis=0, tiled=True)


def collected_together(value, axis):
    leaves = jax.tree.leaves(value)
    order = sorted(range(len(leaves)), key=lambda k: -leaves[k].size)
    width = (1, *leaves[order[0]].shape)[-1]
    lines = [
        jnp.pad(leaves[k].reshape(-1), (0, -leaves[k].size % width)).reshape(-1, width)
        for k in order
    ]
    both, at, found = (from_everyone(jnp.concatenate(lines), axis), 0, {})
    for k, line in zip(order, lines):
        share = both[:, at : at + len(line)].reshape(len(both), -1)
        found[k] = share[:, : leaves[k].size].reshape(-1, *leaves[k].shape)
        at += len(line)
    numbers = iter(range(len(leaves)))
    return jax.tree.map(lambda _: found[next(numbers)], value)


def folded_in_pairs(pieces, combine):
    while len(jax.tree.leaves(pieces)[0]) > 1:
        pieces = jax.vmap(combine)(
            *(jax.tree.map(lambda part: part[side::2], pieces) for side in (0, 1))
        )
    return jax.tree.map(lambda part: part[0], pieces)


def combined_all(value, axis, combine):
    pieces = collected_together(value, axis)
    return folded_in_pairs(pieces, combine)


def once_a_type(value, axis):
    leaves, found = (jax.tree.leaves(value), {})
    for leading, a in enumerate(leaves):
        if leading not in found:
            alike = [k for k, b in enumerate(leaves) if b.dtype == a.dtype]
            got = (
                collected_together([leaves[k] for k in alike], axis)
                if len(alike) > 1
                else [from_everyone(a, axis)]
            )
            for k, b in zip(alike, got):
                found[k] = b
    numbers = iter(range(len(leaves)))
    return jax.tree.map(lambda _: found[next(numbers)], value)


def merged(value, axis, combine):
    pieces = once_a_type(value, axis)
    return folded_in_pairs(pieces, combine)


def combine(first, second):
    top = jnp.maximum(first[0], second[0])
    total = first[1] * jnp.exp(first[0] - top) + second[1] * jnp.exp(second[0] - top)
    return (top, total, first[2] + second[2])


def score_rows(piece, candidates, chosen_targets, owner):
    rows = candidates.shape[0]
    local = chosen_targets - owner * rows
    owned = (local >= 0) & (local < rows)
    chosen = jnp.take(candidates, jnp.clip(local, 0, rows - 1), axis=0)
    products = jnp.sum(piece.astype(jnp.float32) * chosen.astype(jnp.float32), axis=1)
    picked = jnp.where(owned, products, jnp.float32(0.0))
    count = piece.shape[0]
    block = math.gcd(count, 512)
    panels = piece.reshape(count // block, block, piece.shape[1])

    def score_panel(panel):
        scores = jnp.dot(panel, candidates.T, preferred_element_type=jnp.float32)
        peak = jnp.max(scores, axis=1)
        return (peak, jnp.sum(jnp.exp(scores - peak[:, None]), axis=1))

    peaks, sums = lax.map(score_panel, panels)
    return (peaks.reshape(count), sums.reshape(count), picked)


def on_device(queries, candidates, targets):
    owner = lax.axis_index("group") * lax.axis_size(SHARD) + lax.axis_index(SHARD)
    every = gather_axes(queries, GROUP_SHARD, (1, 0, 2, 3), 0)
    top, total, picked = score_rows(every, candidates, targets, owner)
    inner = combined_all((top, total, picked), SHARD, combine)
    top, total, picked = merged(inner, "group", combine)
    losses = top + jnp.log(total) - picked
    return (losses, jnp.mean(losses))


def solution(mesh):
    finer = Mesh(
        mesh.devices.reshape(mesh.shape["group"], 4, 4, 2),
        ("group", "shard_0", "shard_1", "shard_2"),
    )
    in_specs = (P(GROUP_SHARD, None), P(GROUP_SHARD, None), P())
    out_specs = (P(), P())
    return jax.shard_map(
        on_device, mesh=finer, in_specs=in_specs, out_specs=out_specs, check_vma=False
    )
```

profile of v0, /device:TPU:1, one launch (start us, length us, event | category | flops | bytes accessed | tf_op | source)
XLA Modules:
  0.0 195.4 jit_solution(15849809175005774843)
XLA Ops:
  7.2 10.4 %all-gather.1 = bf16[4,6,1024]{2,1,0:T(8,128)(2,1)S(1)} all-gather(bf16[1,6,1024]{2,1,0:T(8,128)(2,1)} %bitcast.56), channel_id=2, replica_groups=mesh['group'=8,'shard_0'=4,'shard_1'=4,'shard_2'=2] {'shard_0'}, dimensions={0}, use_global_device_ids=true | all-gather | bytes 61440 | tf_op jit(solution)/shard_map/all_gather | solution.py:22
  17.6 23.3 %all_gather.13 = bf16[32,6,1024]{2,1,0:T(8,128)(2,1)S(1)} all-gather(bf16[4,6,1024]{2,1,0:T(8,128)(2,1)S(1)} %all-gather.1), channel_id=1, replica_groups=mesh['group'=8,'shard_0'=4,'shard_1'=4,'shard_2'=2] {'group'}, dimensions={0}, use_global_device_ids=true | all-gather | bytes 442368 | tf_op jit(solution)/shard_map/all_gather | solution.py:22
  40.9 1.0 copy.36
  41.9 36.5 %all-gather.5.cloned.1.call-done = bf16[128,6,1024]{2,0,1:T(8,128)(2,1)} async-done(((bf16[32,6,1024]{2,0,1:T(8,128)(2,1)}), bf16[128,6,1024]{2,0,1:T(8,128)(2,1)}) %all-gather.5.cloned.1.call-update) | async-done | bytes 1572880 | tf_op jit(solution)/shard_map/all_gather | solution.py:22
  78.5 0.7 compare_and_fusion
  79.2 11.6 %gather_fusion = bf16[1536,1024]{1,0:T(8,128)(2,1)S(1)} fusion(bf16[4096,1024]{1,0:T(8,128)(2,1)} %param.6, s32[2048]{0:T(1024)S(1)} %pad_clamp_fusion), kind=kCustom, calls=%fused_computation | custom fusion | bytes 6297600 | tf_op jit(solution)/shard_map/jit(_take)/gather | solution.py:99
  90.8 2.9 %gather.7 = bf16[8,4,4,2,6,1024]{5,4,3,2,1,0:T(8,128)(2,1)} reshape(bf16[1536,1024]{1,0:T(8,128)(2,1)S(1)} %gather_fusion) | data formatting | bytes 6291456 | tf_op jit(solution)/shard_map/jit(_take)/gather | solution.py:99
  93.7 0.2 broadcast_in_dim.36
  93.9 0.6 copy.38
  94.5 4.1 %all-gather.7.cloned.1.call-done = bf16[256,6,1024]{2,0,1:T(8,128)(2,1)} async-done(((bf16[128,6,1024]{2,0,1:T(8,128)(2,1)}), bf16[256,6,1024]{2,0,1:T(8,128)(2,1)}) %all-gather.7.cloned.1.call-update) | async-done | bytes 3145744 | tf_op jit(solution)/shard_map/all_gather | solution.py:22
  98.6 4.0 %reshape.57 = bf16[2,4,8,4,6,1024]{5,3,2,1,0,4:T(4,128)(2,1)S(1)} reshape(bf16[256,6,1024]{2,0,1:T(8,128)(2,1)} %all-gather.7.cloned.1.call-done) | data formatting | bytes 6291456 | tf_op jit(solution)/shard_map/reshape | solution.py:24
  102.6 7.8 %multiply_reduce_fusion = f32[8,4,4,2,6]{1,0,2,3,4:T(8,128)S(1)} fusion(bf16[8,4,4,2,6,1024]{5,4,3,2,1,0:T(8,128)(2,1)} %gather.7, pred[8,4,4,2,6]{1,0,2,3,4:T(8,128)(4,1)S(1)} %copy.38, bf16[2,4,8,4,6,1024]{5,3,2,1,0,4:T(4,128)(2,1)S(1)} %reshape.57), kind=kLoop, calls=%fused_computation.6 | loop fusion | flops 7862784 | bytes 6299136 | tf_op jit(solution)/shard_map/reduce_sum | solution.py:100
  110.4 0.5 copy.40
  111.0 0.2 reduce_sum.30
  111.2 3.7 %copy.37 = bf16[8,4,4,2,6,1024]{5,4,3,2,1,0:T(8,128)(2,1)} copy(bf16[8,4,4,2,6,1024]{5,1,0,2,3,4:T(4,128)(2,1)S(1)} %bitcast.43) | data formatting | bytes 6291456 | tf_op jit(solution)/shard_map/transpose | solution.py:26
  115.0 4.9 %reshape_reshape_reshape.3 = bf16[3,512,1024]{2,1,0:T(8,128)(2,1)S(1)} reshape(bf16[8,4,4,2,6,1024]{5,4,3,2,1,0:T(8,128)(2,1)} %copy.37) | data formatting | bytes 6291456 | tf_op jit(solution)/shard_map/reshape;reshape;reshape | solution.py:104
  119.8 25.6 %while.12 = (s32[]{:T(128)}, f32[3,512]{1,0:T(4,128)S(1)}, f32[3,512]{1,0:T(4,128)S(1)}, bf16[3,512,1024]{2,1,0:T(8,128)(2,1)S(1)}, bf16[4096,1024]{1,0:T(8,128)(2,1)}, /*index=5*/s32[]{:T(128)}, s32[]{:T(128)}) while((s32[]{:T(128)}, f32[3,512]{1,0:T(4,128)S(1)}, f32[3,512]{1,0:T(4,128)S(1)}, bf16[3,512,1024]{2,1,0:T(8,128)(2,1)S(1)}, ...), condition=%wide.region_3.4_spmd, body=%wide.region_0.0_spmd.sunk | while | flops 4301257728 | bytes 26228824 | solution.py:111
  119.9 7.1 %fusion.16 = (f32[512]{0:T(512)S(1)}, f32[512,4096]{1,0:T(8,128)S(1)}) fusion(bf16[4096,1024]{1,0:T(8,128)(2,1)} %get-tuple-element.123, bf16[3,512,1024]{2,1,0:T(8,128)(2,1)S(1)} %get-tuple-element.122, s32[]{:T(128)} %get-tuple-element.112), kind=kOutput, calls=%fused_computation.39.clone.1 | convolution fusion | flops 4297063936 | bytes 17827844 | tf_op jit(solution)/shard_map/while/body/eval_jaxpr/dot_general | solution.py:107
  127.0 1.3 exponential_reduce_fusion.2
  128.3 0.1 dynamic_update_slice.9
  128.4 7.1 %fusion.16 = (f32[512]{0:T(512)S(1)}, f32[512,4096]{1,0:T(8,128)S(1)}) fusion(bf16[4096,1024]{1,0:T(8,128)(2,1)} %get-tuple-element.123, bf16[3,512,1024]{2,1,0:T(8,128)(2,1)S(1)} %get-tuple-element.122, s32[]{:T(128)} %get-tuple-element.112), kind=kOutput, calls=%fused_computation.39.clone.1 | convolution fusion | flops 4297063936 | bytes 17827844 | tf_op jit(solution)/shard_map/while/body/eval_jaxpr/dot_general | solution.py:107
  135.5 1.3 exponential_reduce_fusion.2
  136.8 0.1 dynamic_update_slice.9
  136.9 7.1 %fusion.16 = (f32[512]{0:T(512)S(1)}, f32[512,4096]{1,0:T(8,128)S(1)}) fusion(bf16[4096,1024]{1,0:T(8,128)(2,1)} %get-tuple-element.123, bf16[3,512,1024]{2,1,0:T(8,128)(2,1)S(1)} %get-tuple-element.122, s32[]{:T(128)} %get-tuple-element.112), kind=kOutput, calls=%fused_computation.39.clone.1 | convolution fusion | flops 4297063936 | bytes 17827844 | tf_op jit(solution)/shard_map/while/body/eval_jaxpr/dot_general | solution.py:107
  144.0 1.3 exponential_reduce_fusion.2
  145.4 0.1 dynamic_update_slice.9
  145.5 0.1 broadcast_in_dim.41
  145.6 20.8 %all_to_all.10 = f32[32,3,1536]{2,1,0:T(4,128)S(1)} all-to-all(f32[32,3,1536]{2,1,0:T(4,128)S(1)} %broadcast_in_dim.41), channel_id=1, replica_groups=mesh['group'=8,'shard_0'=4,'shard_1'=4,'shard_2'=2] {'shard_0','shard_1'..., dimensions={0} | all-to-all | bytes 1179648 | tf_op jit(solution)/shard_map/all_to_all | solution.py:35
  166.5 0.4 fusion.10
  168.0 17.4 %all_to_all.11 = f32[8,3,1536]{2,1,0:T(4,128)S(1)} all-to-all(f32[8,3,1536]{2,1,0:T(4,128)S(1)} %broadcast_in_dim.42), channel_id=1, replica_groups=mesh['group'=8,'shard_0'=4,'shard_1'=4,'shard_2'=2] {'group'}, dimensions={0} | all-to-all | bytes 294912 | tf_op jit(solution)/shard_map/all_to_all | solution.py:35
  185.5 0.1 fusion.11
  186.0 0.7 fusion.8
  (74 shorter events, 1.7 us)
Async XLA Ops:
  7.2 71.3 %all-gather.5.cloned.1.call-start = ((), (), s32[]{:S(2)}) async-start(), calls=%async_computation.2 | async-start | bytes 1966080 | tf_op jit(solution)/shard_map/all_gather | solution.py:22
  41.9 56.7 %all-gather.7.cloned.1.call-start = ((), (), s32[]{:S(2)}) async-start(), calls=%async_computation.3 | async-start | bytes 4718592 | tf_op jit(solution)/shard_map/all_gather | solution.py:22
  102.6 8.6 %copy-start = (s32[1536]{0:T(1024)S(1)}, s32[1536]{0:T(1024)}, u32[]{:S(2)}) copy-start(s32[1536]{0:T(1024)} %param.7) | copy-start | bytes 18436
Sparse Core Ops, SparseCore 0:
  42.0 36.4 all-gather.4
  80.2 18.3 all-gather.6
where the time goes:
time: 196 us; the launch traced here: 195 us
  blocking collectives  71.9 us (37%)
  waiting for transfers between devices  40.6 us (21%)
  local copies, waits for them, and re-layouts  31.7 us (16%)
  matrix products  21.4 us (11%)
  between operations  16.2 us (8%)
  other arithmetic  13.4 us (7%)
    all_gather x2, waiting for transfers between devices, gather_in_order(): tiles = lax.all_gather(tiles, axes[k], axis=0, tiled=True)  40.6 us
    all_to_all x2, blocking collectives, from_everyone(): return lax.all_to_all(copies, axis, split_axis=0, concat_axis=0, tiled=True)  38.3 us
    all_gather x2, blocking collectives, gather_in_order(): tiles = lax.all_gather(tiles, axes[k], axis=0, tiled=True)  33.7 us
    dot_general x3, matrix products, score_panel(): scores = jnp.dot(panel, candidates.T, preferred_element_type=jnp.float32)  21.4 us
    gather x2, local copies, waits for them, and re-layouts, score_rows(): chosen = jnp.take(candidates, jnp.clip(local, 0, rows - 1), axis=0)  14.5 us
    reduce_sum x1, other arithmetic, score_rows(): jnp.sum(piece.astype(jnp.float32) * chosen.astype(jnp.float32), axis=1)  7.8 us
    another operation x1, local copies, waits for them, and re-layouts, score_rows(): panels = piece.reshape(count // block, block, piece.shape[1])  4.87 us
    reshape x1, local copies, waits for them, and re-layouts, gather_in_order(): tiles = tiles.reshape(*held, *value.shape)  4.01 us
  transfers between devices with their start and end apart: 2, of which 2 were waited for; matrix products, arithmetic and copies ran while one was open for 8% of the time, Pallas kernels for 0%

commit v1 on v0

v1 whole, which is shorter than its diff:
```python
import functools

import jax
import jax.numpy as jnp
from jax import lax
from jax.experimental import pallas as pl
from jax.experimental.pallas import tpu as pltpu
from jax.sharding import Mesh
from jax.sharding import PartitionSpec as P

SHARD = ("x", "y", "core")
EVERY = ("group", *SHARD)
TILE = 512


def broadcast_to_peers(value, axis):
    copies = jnp.broadcast_to(value, (lax.axis_size(axis), *value.shape))
    return lax.all_to_all(copies, axis, split_axis=0, concat_axis=0, tiled=True)


def shifted(value, axis, step):
    size = lax.axis_size(axis)
    return lax.ppermute(value, axis, [(k, (k + step) % size) for k in range(size)])


def score_kernel(tile, queries, candidates, targets, out, scores):
    rows, count = candidates.shape[0], queries.shape[0]
    blocks, groups = rows // tile, tile // 8
    offset = targets[...] - lax.broadcasted_iota(jnp.int32, (8, count), 0)

    def multiply(block, slot):
        part = candidates[pl.ds(pl.multiple_of(block * tile, tile), tile), :]
        scores[slot] = lax.dot_general(
            part, queries[...], (((1,), (1,)), ((), ())), preferred_element_type=jnp.float32
        )

    def fold(block, slot, carry):
        top, total, picked = carry
        here = scores[slot].reshape(groups, 8, count)
        peak = jnp.maximum(top, jnp.max(here, axis=0))
        total = total * jnp.exp(top - peak) + jnp.sum(jnp.exp(here - peak[None]), axis=0)
        local = offset - block * tile
        for k in range(groups):
            picked = jnp.where(local == 8 * k, here[k], picked)
        return peak, total, picked

    def pair(step, carry):
        block = 2 * step
        multiply(block + 1, 1)
        carry = fold(block, 0, carry)
        multiply(block + 2, 0)
        return fold(block + 1, 1, carry)

    zero = jnp.zeros((8, count), jnp.float32)
    carry = (jnp.full((8, count), -jnp.inf, jnp.float32), zero, zero)
    multiply(0, 0)
    carry = lax.fori_loop(0, blocks // 2 - 1, pair, carry)
    multiply(blocks - 1, 1)
    carry = fold(blocks - 2, 0, carry)
    top, total, picked = fold(blocks - 1, 1, carry)
    peak = jnp.max(top, axis=0, keepdims=True)
    total = jnp.sum(total * jnp.exp(top - peak), axis=0, keepdims=True)
    out[0:1, :] = peak + jnp.log(total)
    out[1:2, :] = jnp.sum(picked, axis=0, keepdims=True)


def score(queries, candidates, targets):
    count, width = queries.shape
    rows = candidates.shape[0]
    return pl.pallas_call(
        functools.partial(score_kernel, TILE),
        out_shape=jax.ShapeDtypeStruct((2, count), jnp.float32),
        in_specs=[pl.BlockSpec(memory_space=pltpu.VMEM)] * 3,
        out_specs=pl.BlockSpec(memory_space=pltpu.VMEM),
        scratch_shapes=[pltpu.VMEM((2, TILE, count), jnp.float32)],
        compiler_params=pltpu.CompilerParams(vmem_limit_bytes=16 * 2**20),
        cost_estimate=pl.CostEstimate(
            flops=2 * count * rows * width,
            bytes_accessed=2 * width * (count + rows),
            transcendentals=count * rows,
        ),
        name="score",
    )(queries, candidates, targets.reshape(1, count))


def merge(parts):
    lse, picked = parts[:, 0], parts[:, 1]
    top = jnp.max(lse, axis=0)
    lse = top + jnp.log(jnp.sum(jnp.exp(lse - top), axis=0))
    return jnp.stack([lse, jnp.sum(picked, axis=0)])


def on_device(queries, candidates, targets):
    rows, width = candidates.shape
    at = {axis: lax.axis_index(axis) for axis in EVERY}
    sizes = [lax.axis_size(axis) for axis in EVERY]
    groups, xs, ys, cores = sizes
    each = queries.shape[0]
    owner = 0
    for axis, size in zip(EVERY, sizes):
        owner = owner * size + at[axis]
    local = targets - owner * rows
    local = local.reshape(*sizes, each).transpose(2, 3, 1, 0, 4).reshape(ys, -1)

    line = broadcast_to_peers(queries, "group").reshape(-1, width)
    plane = jnp.zeros((xs, *line.shape), line.dtype)
    plane = lax.dynamic_update_index_in_dim(plane, line, at["x"], 0)
    for step, piece in [(k, shifted(line, "x", k)) for k in (1, xs - 1, 2)]:
        plane = lax.dynamic_update_index_in_dim(plane, piece, (at["x"] - step) % xs, 0)
    plane = plane.reshape(-1, width)

    found = jnp.zeros((ys, 2, cores * plane.shape[0]), jnp.float32)
    steps = (0, 1, ys - 1, 2)
    mine = [plane, *(shifted(plane, "y", k) for k in steps[1:])]
    for step, block in zip(steps, mine):
        other = shifted(block, "core", 1)
        first = jnp.where(at["core"] == 0, block, other)
        second = jnp.where(at["core"] == 0, other, block)
        place = (at["y"] - step) % ys
        chosen = lax.dynamic_index_in_dim(local, place, 0, keepdims=False)
        result = score(jnp.concatenate([first, second]), candidates, chosen)
        found = lax.dynamic_update_index_in_dim(found, result, place, 0)

    partial = found.transpose(1, 0, 2).reshape(2, -1)
    partial = merge(jnp.stack([partial, shifted(partial, "core", 1)]))
    partial = merge(broadcast_to_peers(partial, ("x", "y")))
    lse, picked = merge(broadcast_to_peers(partial, "group"))
    losses = lse - picked
    losses = losses.reshape(ys, cores, xs, groups, each).transpose(3, 2, 0, 1, 4).reshape(-1)
    return (losses, jnp.mean(losses))


def solution(mesh):
    finer = Mesh(mesh.devices.reshape(mesh.shape["group"], 4, 4, 2), EVERY)
    in_specs = (P(EVERY, None), P(EVERY, None), P())
    out_specs = (P(), P())
    return jax.shard_map(
        on_device, mesh=finer, in_specs=in_specs, out_specs=out_specs, check_vma=False
    )
```

time: 196 us -> 103 us (0.53)
  blocking collectives: 71.9 us -> 29.2 us
  waiting for transfers between devices: 40.6 us -> 12.2 us
  starting transfers between devices: 0.08 us -> 27.5 us
  matrix products: 21.4 us -> 0 us
  between operations: 16.2 us -> 2.8 us
  other arithmetic: 13.4 us -> 1.59 us
  local copies, waits for them, and re-layouts: 31.7 us -> 23.5 us
  Pallas kernels: 0 us -> 5.58 us
    all_gather x2 -> x0, waiting for transfers between devices: 40.6 us -> none  [gather_in_order(): tiles = lax.all_gather(tiles, axes[k], axis=0, tiled=True)]
    all_gather x2 -> x0, blocking collectives: 33.7 us -> none  [gather_in_order(): tiles = lax.all_gather(tiles, axes[k], axis=0, tiled=True)]
    dot_general x3 -> x0, matrix products: 21.4 us -> none  [score_panel(): scores = jnp.dot(panel, candidates.T, preferred_element_type=jnp.float32)]
    pallas_call x0 -> x3, local copies, waits for them, and re-layouts: none -> 20.2 us  [score(): pl.pallas_call(functools.partial(score_kernel, TILE), out_shape=jax.Shape...]
    ppermute x0 -> x11, starting transfers between devices: none -> 18.5 us  [shifted(): lax.ppermute(value, axis, [(k, (k + step) % size) for k in range(size)])]
    gather x2 -> x0, local copies, waits for them, and re-layouts: 14.5 us -> none  [score_rows(): chosen = jnp.take(candidates, jnp.clip(local, 0, rows - 1), axis=0)]
    reduce_sum x4 -> x3, other arithmetic: 11.6 us -> 0.09 us  [merge(): lse = top + jnp.log(jnp.sum(jnp.exp(lse - top), axis=0))]
    all_to_all x2, blocking collectives: 38.3 us -> 29.2 us  [broadcast_to_peers(): return lax.all_to_all(copies, axis, split_axis=0, concat_axis=0, tiled=True)]
  transfers between devices with their start and end apart: 2 -> 12, of which waited for: 2 -> 4; matrix products, arithmetic and copies ran while one was open for 8% -> 21% of each run, Pallas kernels for 0% -> 0%
where the time goes in v1:
time: 103 us; the launch traced here: 102 us
  blocking collectives  29.2 us (28%)
  starting transfers between devices  27.5 us (27%)
  local copies, waits for them, and re-layouts  23.5 us (23%)
  waiting for transfers between devices  12.2 us (12%)
  Pallas kernels  5.58 us (5%)
  between operations  2.8 us (3%)
  other arithmetic  1.59 us (2%)
    all_to_all x2, blocking collectives, broadcast_to_peers(): return lax.all_to_all(copies, axis, split_axis=0, concat_axis=0, tiled=True)  29.2 us
    pallas_call x3, local copies, waits for them, and re-layouts, score(): pl.pallas_call(functools.partial(score_kernel, TILE), out_shape=jax.Shape...  20.2 us
    ppermute x11, starting transfers between devices, shifted(): lax.ppermute(value, axis, [(k, (k + step) % size) for k in range(size)])  18.5 us
    all_to_all x1, starting transfers between devices, broadcast_to_peers(): return lax.all_to_all(copies, axis, split_axis=0, concat_axis=0, tiled=True)  9 us
    all_to_all x1, waiting for transfers between devices, broadcast_to_peers(): return lax.all_to_all(copies, axis, split_axis=0, concat_axis=0, tiled=True)  7.75 us
    pallas_call x1, Pallas kernels, score(): pl.pallas_call(functools.partial(score_kernel, TILE), out_shape=jax.Shape...  5.58 us
    ppermute x11, waiting for transfers between devices, shifted(): lax.ppermute(value, axis, [(k, (k + step) % size) for k in range(size)])  4.46 us
  transfers between devices with their start and end apart: 12, of which 4 were waited for; matrix products, arithmetic and copies ran while one was open for 21% of the time, Pallas kernels for 0%

profile of v1, /device:TPU:1, one launch (start us, length us, event | category | flops | bytes accessed | tf_op | source)
XLA Modules:
  0.0 102.4 jit_solution(6260412814888010720)
XLA Ops:
  0.6 1.4 %broadcast_in_dim.46 = bf16[8,6,1024]{2,1,0:T(8,128)(2,1)} broadcast(bf16[6,1024]{1,0:T(8,128)(2,1)} %param.3), dimensions={1,2} | broadcast | bytes 110592 | tf_op jit(solution)/shard_map/broadcast_in_dim | solution.py:17
  2.0 9.0 %all-to-all-start = ((bf16[8,6,1024]{2,1,0:T(8,128)(2,1)}), bf16[8,6,1024]{2,1,0:T(8,128)(2,1)S(1)}, u32[]{:S(2)}, u32[]{:S(2)}) async-start(bf16[8,6,1024]{2,1,0:T(8,128)(2,1)} %broadcast_in_dim.46), calls=%async_computation | async-start | bytes 262144 | tf_op jit(solution)/shard_map/all_to_all | solution.py:18
  11.0 7.8 %all-to-all-done = bf16[8,6,1024]{2,1,0:T(8,128)(2,1)S(1)} async-done(((bf16[8,6,1024]{2,1,0:T(8,128)(2,1)}), bf16[8,6,1024]{2,1,0:T(8,128)(2,1)S(1)}, u32[]{:S(2)}, u32[]{:S(2)}) %all-to-all-start) | async-done | bytes 98336 | tf_op jit(solution)/shard_map/all_to_all | solution.py:18
  18.8 1.3 %collective-permute-start = (bf16[48,1024]{1,0:T(8,128)(2,1)S(1)}, bf16[48,1024]{1,0:T(8,128)(2,1)S(1)}, u32[]{:S(2)}, u32[]{:S(2)}) collective-permute-start(bf16[48,1024]{1,0:T(8,128)(2,1)S(1)} %reshape.69), channel_id=1, source_target_pairs={{0,8},{8,16},{16,24},{24,0},{1,9},{9,17},{17,25},{25,1},{2,10},{10... | collective-permute-start | bytes 294920 | tf_op jit(solution)/shard_map/ppermute | solution.py:23
  20.1 1.5 %collective-permute-start.1 = (bf16[48,1024]{1,0:T(8,128)(2,1)S(1)}, bf16[48,1024]{1,0:T(8,128)(2,1)S(1)}, u32[]{:S(2)}, u32[]{:S(2)}) collective-permute-start(bf16[48,1024]{1,0:T(8,128)(2,1)S(1)} %reshape.69), channel_id=1, source_target_pairs={{0,24},{8,0},{16,8},{24,16},{1,25},{9,1},{17,9},{25,17},{2,26},{10... | collective-permute-start | bytes 294920 | tf_op jit(solution)/shard_map/ppermute | solution.py:23
  21.6 1.5 %collective-permute-start.2 = (bf16[48,1024]{1,0:T(8,128)(2,1)S(1)}, bf16[48,1024]{1,0:T(8,128)(2,1)S(1)}, u32[]{:S(2)}, u32[]{:S(2)}) collective-permute-start(bf16[48,1024]{1,0:T(8,128)(2,1)S(1)} %reshape.69), channel_id=1, source_target_pairs={{0,16},{8,24},{16,0},{24,8},{1,17},{9,25},{17,1},{25,9},{2,18},{10... | collective-permute-start | bytes 294920 | tf_op jit(solution)/shard_map/ppermute | solution.py:23
  23.2 0.4 collective-permute-done
  23.6 3.2 %collective-permute-done.2 = bf16[48,1024]{1,0:T(8,128)(2,1)S(1)} collective-permute-done((bf16[48,1024]{1,0:T(8,128)(2,1)S(1)}, bf16[48,1024]{1,0:T(8,128)(2,1)S(1)}, u32[]{:S(2)}, u32[]{:S(2)}) %collective-permute-start.2) | collective-permute-done | bytes 98336 | tf_op jit(solution)/shard_map/ppermute | solution.py:23
  26.8 1.4 %collective-permute-start.4 = (bf16[192,1024]{1,0:T(8,128)(2,1)S(1)}, bf16[192,1024]{1,0:T(8,128)(2,1)S(1)}, u32[]{:S(2)}, u32[]{:S(2)}) collective-permute-start(bf16[192,1024]{1,0:T(8,128)(2,1)S(1)} %bitcast.44), channel_id=1, source_target_pairs={{0,2},{2,4},{4,6},{6,0},{1,3},{3,5},{5,7},{7,1},{8,10},{10,12},{12... | collective-permute-start | bytes 1179656 | tf_op jit(solution)/shard_map/ppermute | solution.py:23
  28.2 4.0 %collective-permute-start.3 = (bf16[192,1024]{1,0:T(8,128)(2,1)S(1)}, bf16[192,1024]{1,0:T(8,128)(2,1)S(1)}, u32[]{:S(2)}, u32[]{:S(2)}) collective-permute-start(bf16[192,1024]{1,0:T(8,128)(2,1)S(1)} %bitcast.45), channel_id=1, source_target_pairs={{0,1},{1,0},{2,3},{3,2},{4,5},{5,4},{6,7},{7,6},{8,9},{9,8},{10,11... | collective-permute-start | bytes 1179656 | tf_op jit(solution)/shard_map/ppermute | solution.py:23
  32.2 0.2 reshape.71
  32.4 0.1 copy.11
  32.5 0.1 reshape.72
  32.7 1.5 %collective-permute-start.6 = (bf16[192,1024]{1,0:T(8,128)(2,1)S(1)}, bf16[192,1024]{1,0:T(8,128)(2,1)S(1)}, u32[]{:S(2)}, u32[]{:S(2)}) collective-permute-start(bf16[192,1024]{1,0:T(8,128)(2,1)S(1)} %bitcast.46), channel_id=1, source_target_pairs={{0,6},{2,0},{4,2},{6,4},{1,7},{3,1},{5,3},{7,5},{8,14},{10,8},{12,... | collective-permute-start | bytes 1179656 | tf_op jit(solution)/shard_map/ppermute | solution.py:23
  34.2 1.7 %collective-permute-start.8 = (bf16[192,1024]{1,0:T(8,128)(2,1)S(1)}, bf16[192,1024]{1,0:T(8,128)(2,1)S(1)}, u32[]{:S(2)}, u32[]{:S(2)}) collective-permute-start(bf16[192,1024]{1,0:T(8,128)(2,1)S(1)} %bitcast.47), channel_id=1, source_target_pairs={{0,4},{2,6},{4,0},{6,2},{1,5},{3,7},{5,1},{7,3},{8,12},{10,14},{12... | collective-permute-start | bytes 1179656 | tf_op jit(solution)/shard_map/ppermute | solution.py:23
  35.9 4.8 %collective-permute-start.5 = (bf16[192,1024]{1,0:T(8,128)(2,1)S(1)}, bf16[192,1024]{1,0:T(8,128)(2,1)S(1)}, u32[]{:S(2)}, u32[]{:S(2)}) collective-permute-start(bf16[192,1024]{1,0:T(8,128)(2,1)S(1)} %collective-permute-done.4), channel_id=1, source_target_pairs={{0,1},{1,0},{2,3},{3,2},{4,5},{5,4},{6,7},{7,6},{8,9},{9,8},{10,11... | collective-permute-start | bytes 1179656 | tf_op jit(solution)/shard_map/ppermute | solution.py:23
  40.8 9.0 %score.7 = f32[4,2,384]{2,1,0:T(2,128)S(1)} fusion(f32[4,2,384]{2,1,0:T(2,128)S(1)} %broadcast_in_dim.44, s32[]{:T(128)S(6)} %select_n.109, bf16[384,1024]{1,0:T(8,128)(2,1)S(1)} %pad_maximum_fusion, bf16[4096,1024]{1,0:T(8,128)(2,1)} %candidates.4, s32[1,384]{1,0:T(1,128)S(1)} %get-tuple-element.24), kind=kCustom, calls=%fused_computation.39 | custom fusion | bytes 9179652 | tf_op jit(solution)/shard_map/score/pallas_call | solution.py:70
  49.8 0.1 collective-permute-start.7
  49.9 0.5 collective-permute-start.9
  50.6 5.6 %score.6 = f32[4,2,384]{2,1,0:T(2,128)S(1)} fusion(f32[4,2,384]{2,1,0:T(2,128)S(1)} %score.7, s32[]{:T(128)S(6)} %select_n.113, bf16[384,1024]{1,0:T(8,128)(2,1)S(1)} %pad_maximum_fusion.1, bf16[4096,1024]{1,0:T(8,128)(2,1)S(1)} %bitcast.43, s32[1,384]{1,0:T(1,128)S(1)} %get-tuple-element.23), kind=kCustom, calls=%fused_computation.38 | custom fusion | bytes 9179652 | tf_op jit(solution)/shard_map/score/pallas_call | solution.py:70
  56.3 5.6 %score.5 = f32[4,2,384]{2,1,0:T(2,128)S(1)} fusion(f32[4,2,384]{2,1,0:T(2,128)S(1)} %score.6, s32[]{:T(128)S(6)} %select_n.117, bf16[384,1024]{1,0:T(8,128)(2,1)S(1)} %pad_maximum_fusion.2, bf16[4096,1024]{1,0:T(8,128)(2,1)S(1)} %bitcast.43, s32[1,384]{1,0:T(1,128)S(1)} %get-tuple-element.22), kind=kCustom, calls=%fused_computation.37 | custom fusion | bytes 9179652 | tf_op jit(solution)/shard_map/score/pallas_call | solution.py:70
  62.1 5.6 %score.4 = f32[2,384]{1,0:T(2,128)S(1)} custom-call(bf16[384,1024]{1,0:T(8,128)(2,1)S(1)} %pad_maximum_fusion.3.queries, bf16[4096,1024]{1,0:T(8,128)(2,1)S(1)} %bitcast.43, s32[1,384]{1,0:T(1,128)S(1)} %get-tuple-element.21.targets), custom_call_target="tpu_custom_call" | custom-call | flops 3221225472 | bytes 9175040 | tf_op jit(solution)/shard_map/score/pallas_call | solution.py:70
  67.7 0.4 collective-permute-start.10
  68.1 0.9 collective-permute-done.10
  69.2 19.1 %all_to_all.15 = f32[16,2,1536]{2,1,0:T(2,128)S(1)} all-to-all(f32[16,2,1536]{2,1,0:T(2,128)S(1)} %broadcast_in_dim.55), channel_id=1, replica_groups=mesh['group'=8,'x'=4,'y'=4,'core'=2] {'x','y'}, dimensions={0} | all-to-all | bytes 393216 | tf_op jit(solution)/shard_map/all_to_all | solution.py:18
  88.4 0.2 slice_reduce_fusion.3
  88.7 10.1 %all_to_all.16 = f32[8,2,1536]{2,1,0:T(2,128)S(1)} all-to-all(f32[8,2,1536]{2,1,0:T(2,128)S(1)} %broadcast_in_dim.56), channel_id=1, replica_groups=mesh['group'=8,'x'=4,'y'=4,'core'=2] {'group'}, dimensions={0} | all-to-all | bytes 196608 | tf_op jit(solution)/shard_map/all_to_all | solution.py:18
  98.8 0.1 slice_reduce_fusion.2
  98.9 0.6 fusion.8
  99.5 0.1 sub.71
  99.7 0.1 copy.18
  99.8 0.8 reshape.74
  (53 shorter events, 1.1 us)
Async XLA Ops:
  0.6 31.6 %copy-start = (s32[1536]{0:T(1024)S(1)}, s32[1536]{0:T(1024)}, u32[]{:S(2)}) copy-start(s32[1536]{0:T(1024)} %param.5) | copy-start | bytes 18436
  2.0 16.8 %all-to-all-start = ((bf16[8,6,1024]{2,1,0:T(8,128)(2,1)}), bf16[8,6,1024]{2,1,0:T(8,128)(2,1)S(1)}, u32[]{:S(2)}, u32[]{:S(2)}) async-start(bf16[8,6,1024]{2,1,0:T(8,128)(2,1)} %broadcast_in_dim.46), calls=%async_computation | async-start | bytes 262144 | tf_op jit(solution)/shard_map/all_to_all | solution.py:18
  18.8 4.8 %collective-permute-start = (bf16[48,1024]{1,0:T(8,128)(2,1)S(1)}, bf16[48,1024]{1,0:T(8,128)(2,1)S(1)}, u32[]{:S(2)}, u32[]{:S(2)}) collective-permute-start(bf16[48,1024]{1,0:T(8,128)(2,1)S(1)} %reshape.69), channel_id=1, source_target_pairs={{0,8},{8,16},{16,24},{24,0},{1,9},{9,17},{17,25},{25,1},{2,10},{10... | collective-permute-start | bytes 294920 | tf_op jit(solution)/shard_map/ppermute | solution.py:23
  20.1 3.5 %collective-permute-start.1 = (bf16[48,1024]{1,0:T(8,128)(2,1)S(1)}, bf16[48,1024]{1,0:T(8,128)(2,1)S(1)}, u32[]{:S(2)}, u32[]{:S(2)}) collective-permute-start(bf16[48,1024]{1,0:T(8,128)(2,1)S(1)} %reshape.69), channel_id=1, source_target_pairs={{0,24},{8,0},{16,8},{24,16},{1,25},{9,1},{17,9},{25,17},{2,26},{10... | collective-permute-start | bytes 294920 | tf_op jit(solution)/shard_map/ppermute | solution.py:23
  21.6 5.3 %collective-permute-start.2 = (bf16[48,1024]{1,0:T(8,128)(2,1)S(1)}, bf16[48,1024]{1,0:T(8,128)(2,1)S(1)}, u32[]{:S(2)}, u32[]{:S(2)}) collective-permute-start(bf16[48,1024]{1,0:T(8,128)(2,1)S(1)} %reshape.69), channel_id=1, source_target_pairs={{0,16},{8,24},{16,0},{24,8},{1,17},{9,25},{17,1},{25,9},{2,18},{10... | collective-permute-start | bytes 294920 | tf_op jit(solution)/shard_map/ppermute | solution.py:23
  26.8 9.1 %collective-permute-start.4 = (bf16[192,1024]{1,0:T(8,128)(2,1)S(1)}, bf16[192,1024]{1,0:T(8,128)(2,1)S(1)}, u32[]{:S(2)}, u32[]{:S(2)}) collective-permute-start(bf16[192,1024]{1,0:T(8,128)(2,1)S(1)} %bitcast.44), channel_id=1, source_target_pairs={{0,2},{2,4},{4,6},{6,0},{1,3},{3,5},{5,7},{7,1},{8,10},{10,12},{12... | collective-permute-start | bytes 1179656 | tf_op jit(solution)/shard_map/ppermute | solution.py:23
  28.2 12.4 %collective-permute-start.3 = (bf16[192,1024]{1,0:T(8,128)(2,1)S(1)}, bf16[192,1024]{1,0:T(8,128)(2,1)S(1)}, u32[]{:S(2)}, u32[]{:S(2)}) collective-permute-start(bf16[192,1024]{1,0:T(8,128)(2,1)S(1)} %bitcast.45), channel_id=1, source_target_pairs={{0,1},{1,0},{2,3},{3,2},{4,5},{5,4},{6,7},{7,6},{8,9},{9,8},{10,11... | collective-permute-start | bytes 1179656 | tf_op jit(solution)/shard_map/ppermute | solution.py:23
  32.7 17.1 %collective-permute-start.6 = (bf16[192,1024]{1,0:T(8,128)(2,1)S(1)}, bf16[192,1024]{1,0:T(8,128)(2,1)S(1)}, u32[]{:S(2)}, u32[]{:S(2)}) collective-permute-start(bf16[192,1024]{1,0:T(8,128)(2,1)S(1)} %bitcast.46), channel_id=1, source_target_pairs={{0,6},{2,0},{4,2},{6,4},{1,7},{3,1},{5,3},{7,5},{8,14},{10,8},{12,... | collective-permute-start | bytes 1179656 | tf_op jit(solution)/shard_map/ppermute | solution.py:23
  34.2 15.8 %collective-permute-start.8 = (bf16[192,1024]{1,0:T(8,128)(2,1)S(1)}, bf16[192,1024]{1,0:T(8,128)(2,1)S(1)}, u32[]{:S(2)}, u32[]{:S(2)}) collective-permute-start(bf16[192,1024]{1,0:T(8,128)(2,1)S(1)} %bitcast.47), channel_id=1, source_target_pairs={{0,4},{2,6},{4,0},{6,2},{1,5},{3,7},{5,1},{7,3},{8,12},{10,14},{12... | collective-permute-start | bytes 1179656 | tf_op jit(solution)/shard_map/ppermute | solution.py:23
  35.9 14.5 %collective-permute-start.5 = (bf16[192,1024]{1,0:T(8,128)(2,1)S(1)}, bf16[192,1024]{1,0:T(8,128)(2,1)S(1)}, u32[]{:S(2)}, u32[]{:S(2)}) collective-permute-start(bf16[192,1024]{1,0:T(8,128)(2,1)S(1)} %collective-permute-done.4), channel_id=1, source_target_pairs={{0,1},{1,0},{2,3},{3,2},{4,5},{5,4},{6,7},{7,6},{8,9},{9,8},{10,11... | collective-permute-start | bytes 1179656 | tf_op jit(solution)/shard_map/ppermute | solution.py:23
  40.7 9.8 %slice-start = ((s8[8388608]{0:T(1024)(128)(4,1)}), s8[4194304]{0:T(1024)(128)(4,1)S(1)}, s32[]{:S(2)}) async-start(s8[8388608]{0:T(1024)(128)(4,1)} %bitcast.42), calls=%async_computation.3 | async-start | bytes 8388608
  40.8 9.8 %slice-start.1 = ((s8[8388608]{0:T(1024)(128)(4,1)}), s8[4194304]{0:T(1024)(128)(4,1)S(1)}, s32[]{:S(2)}) async-start(s8[8388608]{0:T(1024)(128)(4,1)} %bitcast.42), calls=%async_computation.4 | async-start | bytes 8388608
  49.8 6.4 %collective-permute-start.7 = (bf16[192,1024]{1,0:T(8,128)(2,1)S(1)}, bf16[192,1024]{1,0:T(8,128)(2,1)S(1)}, u32[]{:S(2)}, u32[]{:S(2)}) collective-permute-start(bf16[192,1024]{1,0:T(8,128)(2,1)S(1)} %collective-permute-done.6), channel_id=1, source_target_pairs={{0,1},{1,0},{2,3},{3,2},{4,5},{5,4},{6,7},{7,6},{8,9},{9,8},{10,11... | collective-permute-start | bytes 1179656 | tf_op jit(solution)/shard_map/ppermute | solution.py:23
  49.9 12.0 %collective-permute-start.9 = (bf16[192,1024]{1,0:T(8,128)(2,1)S(1)}, bf16[192,1024]{1,0:T(8,128)(2,1)S(1)}, u32[]{:S(2)}, u32[]{:S(2)}) collective-permute-start(bf16[192,1024]{1,0:T(8,128)(2,1)S(1)} %collective-permute-done.8), channel_id=1, source_target_pairs={{0,1},{1,0},{2,3},{3,2},{4,5},{5,4},{6,7},{7,6},{8,9},{9,8},{10,11... | collective-permute-start | bytes 1179656 | tf_op jit(solution)/shard_map/ppermute | solution.py:23
  67.7 1.3 %collective-permute-start.10 = (f32[2,1536]{1,0:T(2,128)S(1)}, f32[2,1536]{1,0:T(2,128)S(1)}, u32[]{:S(2)}, u32[]{:S(2)}) collective-permute-start(f32[2,1536]{1,0:T(2,128)S(1)} %bitcast.52), channel_id=1, source_target_pairs={{0,1},{1,0},{2,3},{3,2},{4,5},{5,4},{6,7},{7,6},{8,9},{9,8},{10,11... | collective-permute-start | bytes 36872 | tf_op jit(solution)/shard_map/ppermute | solution.py:23

commit v2 on v1

v2 whole, which is shorter than its diff:
```python
import functools

import jax
import jax.numpy as jnp
from jax import lax
from jax.experimental import pallas as pl
from jax.experimental.pallas import tpu as pltpu
from jax.sharding import Mesh
from jax.sharding import PartitionSpec as P

SHARD = ("x", "y", "core")
EVERY = ("group", *SHARD)
TILE = 512


def broadcast_to_peers(value, axis):
    copies = jnp.broadcast_to(value, (lax.axis_size(axis), *value.shape))
    return lax.all_to_all(copies, axis, split_axis=0, concat_axis=0, tiled=True)


def shifted(value, axis, step):
    size = lax.axis_size(axis)
    return lax.ppermute(value, axis, [(k, (k + step) % size) for k in range(size)])


def turned(axis):
    size = lax.axis_size(axis)
    at = lax.axis_index(axis).astype(jnp.uint32)
    return [lax.rem(at + jnp.uint32(size - k), jnp.uint32(size)) for k in range(size)]


def score_kernel(tiles, queries, candidates, targets, out, scores, *stream):
    count = queries.shape[0]
    starts = [sum(tiles[:k]) for k in range(len(tiles))]
    places = [pl.ds(start, tile) for start, tile in zip(starts, tiles)]
    local = targets[...] - lax.broadcasted_iota(jnp.int32, (8, count), 0)
    source, copies = candidates, {}
    if stream:
        source, sems = stream
        cuts = [0, starts[1], starts[len(tiles) // 2], candidates.shape[0]]
        for k, (start, end) in enumerate(zip(cuts, cuts[1:])):
            part = pl.ds(start, end - start)
            copy = pltpu.make_async_copy(candidates.at[part], source.at[part], sems.at[k])
            copy.start()
            copies[starts.index(start)] = copy

    def multiply(k):
        if k in copies:
            copies[k].wait()
        scores[k % 2, : tiles[k]] = lax.dot_general(
            source[places[k], :],
            queries[...],
            (((1,), (1,)), ((), ())),
            preferred_element_type=jnp.float32,
        )

    top = jnp.full((8, count), -jnp.inf, jnp.float32)
    total = picked = jnp.zeros((8, count), jnp.float32)
    multiply(0)
    for k, tile in enumerate(tiles):
        if k + 1 < len(tiles):
            multiply(k + 1)
        here = scores[k % 2, :tile].reshape(tile // 8, 8, count)
        peak = jnp.maximum(top, jnp.max(here, axis=0))
        total = total * jnp.exp(top - peak) + jnp.sum(jnp.exp(here - peak[None]), axis=0)
        top = peak
        for row in range(tile // 8):
            picked = jnp.where(local == starts[k] + 8 * row, here[row], picked)
    peak = jnp.max(top, axis=0, keepdims=True)
    total = jnp.sum(total * jnp.exp(top - peak), axis=0, keepdims=True)
    out[0:1, :] = peak + jnp.log(total)
    out[1:2, :] = jnp.sum(picked, axis=0, keepdims=True)


def score(queries, candidates, targets, streamed=False):
    count, width = queries.shape
    rows = candidates.shape[0]
    tiles = [TILE // 2] + [TILE] * (rows // TILE - 1) + [TILE // 2]
    scratch = [pltpu.VMEM((2, TILE, count), jnp.float32)]
    if streamed:
        scratch += [
            pltpu.VMEM(candidates.shape, candidates.dtype),
            pltpu.SemaphoreType.DMA((3,)),
        ]
    vmem = pl.BlockSpec(memory_space=pltpu.VMEM)
    return pl.pallas_call(
        functools.partial(score_kernel, tiles),
        out_shape=jax.ShapeDtypeStruct((2, count), jnp.float32),
        in_specs=[vmem, pl.BlockSpec(memory_space=pl.ANY) if streamed else vmem, vmem],
        out_specs=vmem,
        scratch_shapes=scratch,
        compiler_params=pltpu.CompilerParams(
            vmem_limit_bytes=(50 if streamed else 16) * 2**20
        ),
        cost_estimate=pl.CostEstimate(
            flops=2 * count * rows * width,
            bytes_accessed=2 * width * (count + rows),
            transcendentals=count * rows,
        ),
        name="score",
    )(queries, candidates, targets)


def merge(parts):
    lse, picked = parts[:, 0], parts[:, 1]
    top = jnp.max(lse, axis=0)
    lse = top + jnp.log(jnp.sum(jnp.exp(lse - top), axis=0))
    return jnp.stack([lse, jnp.sum(picked, axis=0)])


def on_device(queries, candidates, targets):
    rows, width = candidates.shape
    at = {axis: lax.axis_index(axis) for axis in EVERY}
    sizes = [lax.axis_size(axis) for axis in EVERY]
    groups, xs, ys, cores = sizes
    each = queries.shape[0]
    owner = 0
    for axis, size in zip(EVERY, sizes):
        owner = owner * size + at[axis]

    local = targets - owner * rows
    local = local.reshape(*sizes, each).transpose(2, 3, 1, 0, 4).reshape(ys, -1)
    x_place = turned("x")
    y_place = turned("y")
    line = broadcast_to_peers(queries, "group").reshape(-1, width)
    line, local, x_place, y_place, even = lax.optimization_barrier(
        (line, local, x_place, y_place, at["core"] == 0)
    )
    pieces = [(k, shifted(line, "x", k)) for k in (1, xs - 1, 2)]
    plane = jnp.zeros((xs, *line.shape), line.dtype)
    plane = lax.dynamic_update_index_in_dim(plane, line, x_place[0], 0)
    for step, piece in pieces:
        plane = lax.dynamic_update_index_in_dim(plane, piece, x_place[step], 0)
    plane = plane.reshape(-1, width)
    chosen = [lax.dynamic_slice_in_dim(local, place, 1, 0) for place in y_place]

    def chip(block):
        other = shifted(block, "core", 1)
        return jnp.concatenate([jnp.where(even, block, other), jnp.where(even, other, block)])

    near = [shifted(plane, "y", k) for k in (1, ys - 1)]
    mine = score(chip(plane), candidates, chosen[0], True)
    half = plane.shape[0] // 2
    far = [shifted(near[0][:half], "y", 1), shifted(near[1][half:], "y", ys - 1)]
    beside = score(
        jnp.concatenate([chip(block) for block in near]),
        candidates,
        jnp.concatenate([chosen[1], chosen[3]], axis=1),
    )
    last = score(chip(jnp.concatenate(far)), candidates, chosen[2])

    mine, beside, last = lax.optimization_barrier((mine, beside, last))
    found = jnp.zeros((2, ys, last.shape[1]), jnp.float32)
    parts = [(0, mine), (1, beside[:, : last.shape[1]]), (ys - 1, beside[:, last.shape[1] :]), (2, last)]
    for step, part in parts:
        found = lax.dynamic_update_index_in_dim(found, part, y_place[step], 1)
    partial = found.reshape(2, -1)
    partial = merge(jnp.stack([partial, shifted(partial, "core", 1)]))
    partial = merge(broadcast_to_peers(partial, ("x", "y")))
    lse, picked = merge(broadcast_to_peers(partial, "group"))
    losses = lse - picked
    losses = losses.reshape(ys, cores, xs, groups, each).transpose(3, 2, 0, 1, 4).reshape(-1)
    return (losses, jnp.mean(losses))


def solution(mesh):
    finer = Mesh(mesh.devices.reshape(mesh.shape["group"], 4, 4, 2), EVERY)
    in_specs = (P(EVERY, None), P(EVERY, None), P())
    out_specs = (P(), P())
    return jax.shard_map(
        on_device, mesh=finer, in_specs=in_specs, out_specs=out_specs, check_vma=False
    )
```

time: 103 us -> 93.2 us (0.905)
  local copies, waits for them, and re-layouts: 23.5 us -> 3.27 us
  Pallas kernels: 5.58 us -> 19.6 us
  blocking collectives: 29.2 us -> 21.4 us
  starting transfers between devices: 27.5 us -> 29.5 us
  waiting for transfers between devices: 12.2 us -> 13.3 us
    pallas_call x3 -> x0, local copies, waits for them, and re-layouts: 20.2 us -> none  [score(): pl.pallas_call(functools.partial(score_kernel, TILE), out_shape=jax.Shape...]
    pallas_call x1 -> x3, Pallas kernels: 5.58 us -> 19.6 us  [score(): pl.pallas_call(functools.partial(score_kernel, tiles), out_shape=jax.Shap...]
    all_to_all x2, blocking collectives: 29.2 us -> 21.4 us  [broadcast_to_peers(): return lax.all_to_all(copies, axis, split_axis=0, concat_axis=0, tiled=True)]
    ppermute x11 -> x12, waiting for transfers between devices: 4.46 us -> 6.77 us  [shifted(): lax.ppermute(value, axis, [(k, (k + step) % size) for k in range(size)])]
    ppermute x11 -> x12, starting transfers between devices: 18.5 us -> 20.5 us  [shifted(): lax.ppermute(value, axis, [(k, (k + step) % size) for k in range(size)])]
    all_to_all x1, waiting for transfers between devices: 7.75 us -> 6.57 us  [broadcast_to_peers(): return lax.all_to_all(copies, axis, split_axis=0, concat_axis=0, tiled=True)]
  transfers between devices with their start and end apart: 12 -> 13, of which waited for: 4 -> 6; matrix products, arithmetic and copies ran while one was open for 21% -> 2% of each run, Pallas kernels for 0% -> 16%
where the time goes in v2:
time: 93.2 us; the launch traced here: 92.4 us
  starting transfers between devices  29.5 us (32%)
  blocking collectives  21.4 us (23%)
  Pallas kernels  19.6 us (21%)
  waiting for transfers between devices  13.3 us (14%)
  local copies, waits for them, and re-layouts  3.27 us (4%)
  between operations  2.82 us (3%)
  other arithmetic  2.34 us (3%)
    all_to_all x2, blocking collectives, broadcast_to_peers(): return lax.all_to_all(copies, axis, split_axis=0, concat_axis=0, tiled=True)  21.4 us
    ppermute x12, starting transfers between devices, shifted(): lax.ppermute(value, axis, [(k, (k + step) % size) for k in range(size)])  20.5 us
    pallas_call x3, Pallas kernels, score(): pl.pallas_call(functools.partial(score_kernel, tiles), out_shape=jax.Shap...  19.6 us
    all_to_all x1, starting transfers between devices, broadcast_to_peers(): return lax.all_to_all(copies, axis, split_axis=0, concat_axis=0, tiled=True)  9 us
    ppermute x12, waiting for transfers between devices, shifted(): lax.ppermute(value, axis, [(k, (k + step) % size) for k in range(size)])  6.77 us
    all_to_all x1, waiting for transfers between devices, broadcast_to_peers(): return lax.all_to_all(copies, axis, split_axis=0, concat_axis=0, tiled=True)  6.57 us
  transfers between devices with their start and end apart: 13, of which 6 were waited for; matrix products, arithmetic and copies ran while one was open for 2% of the time, Pallas kernels for 16%

profile of v2, /device:TPU:1, one launch (start us, length us, event | category | flops | bytes accessed | tf_op | source)
XLA Modules:
  0.0 92.4 jit_solution(9518896686226798428)
XLA Ops:
  0.6 1.4 %broadcast_in_dim.45 = bf16[8,6,1024]{2,1,0:T(8,128)(2,1)} broadcast(bf16[6,1024]{1,0:T(8,128)(2,1)} %param.3), dimensions={1,2} | broadcast | bytes 110592 | tf_op jit(solution)/shard_map/broadcast_in_dim | solution.py:17
  2.0 9.0 %all-to-all-start = ((bf16[8,6,1024]{2,1,0:T(8,128)(2,1)}), bf16[8,6,1024]{2,1,0:T(8,128)(2,1)S(1)}, u32[]{:S(2)}, u32[]{:S(2)}) async-start(bf16[8,6,1024]{2,1,0:T(8,128)(2,1)} %broadcast_in_dim.45), calls=%async_computation | async-start | bytes 262144 | tf_op jit(solution)/shard_map/all_to_all | solution.py:18
  11.0 0.7 broadcast_subtract_fusion
  11.7 0.2 reshape.65
  12.0 0.1 reshape.66
  12.2 6.6 %all-to-all-done = bf16[8,6,1024]{2,1,0:T(8,128)(2,1)S(1)} async-done(((bf16[8,6,1024]{2,1,0:T(8,128)(2,1)}), bf16[8,6,1024]{2,1,0:T(8,128)(2,1)S(1)}, u32[]{:S(2)}, u32[]{:S(2)}) %all-to-all-start) | async-done | bytes 98336 | tf_op jit(solution)/shard_map/all_to_all | solution.py:18
  18.8 1.3 %collective-permute-start = (bf16[48,1024]{1,0:T(8,128)(2,1)S(1)}, bf16[48,1024]{1,0:T(8,128)(2,1)S(1)}, u32[]{:S(2)}, u32[]{:S(2)}) collective-permute-start(bf16[48,1024]{1,0:T(8,128)(2,1)S(1)} %reshape.64), channel_id=1, source_target_pairs={{0,8},{8,16},{16,24},{24,0},{1,9},{9,17},{17,25},{25,1},{2,10},{10... | collective-permute-start | bytes 294920 | tf_op jit(solution)/shard_map/ppermute | solution.py:23
  20.1 1.5 %collective-permute-start.1 = (bf16[48,1024]{1,0:T(8,128)(2,1)S(1)}, bf16[48,1024]{1,0:T(8,128)(2,1)S(1)}, u32[]{:S(2)}, u32[]{:S(2)}) collective-permute-start(bf16[48,1024]{1,0:T(8,128)(2,1)S(1)} %reshape.64), channel_id=1, source_target_pairs={{0,24},{8,0},{16,8},{24,16},{1,25},{9,1},{17,9},{25,17},{2,26},{10... | collective-permute-start | bytes 294920 | tf_op jit(solution)/shard_map/ppermute | solution.py:23
  21.5 1.5 %collective-permute-start.2 = (bf16[48,1024]{1,0:T(8,128)(2,1)S(1)}, bf16[48,1024]{1,0:T(8,128)(2,1)S(1)}, u32[]{:S(2)}, u32[]{:S(2)}) collective-permute-start(bf16[48,1024]{1,0:T(8,128)(2,1)S(1)} %reshape.64), channel_id=1, source_target_pairs={{0,16},{8,24},{16,0},{24,8},{1,17},{9,25},{17,1},{25,9},{2,18},{10... | collective-permute-start | bytes 294920 | tf_op jit(solution)/shard_map/ppermute | solution.py:23
  23.1 0.4 collective-permute-done
  23.6 3.2 %collective-permute-done.2 = bf16[48,1024]{1,0:T(8,128)(2,1)S(1)} collective-permute-done((bf16[48,1024]{1,0:T(8,128)(2,1)S(1)}, bf16[48,1024]{1,0:T(8,128)(2,1)S(1)}, u32[]{:S(2)}, u32[]{:S(2)}) %collective-permute-start.2) | collective-permute-done | bytes 98336 | tf_op jit(solution)/shard_map/ppermute | solution.py:23
  26.8 1.4 %collective-permute-start.4 = (bf16[192,1024]{1,0:T(8,128)(2,1)S(1)}, bf16[192,1024]{1,0:T(8,128)(2,1)S(1)}, u32[]{:S(2)}, u32[]{:S(2)}) collective-permute-start(bf16[192,1024]{1,0:T(8,128)(2,1)S(1)} %bitcast.45), channel_id=1, source_target_pairs={{0,2},{2,4},{4,6},{6,0},{1,3},{3,5},{5,7},{7,1},{8,10},{10,12},{12... | collective-permute-start | bytes 1179656 | tf_op jit(solution)/shard_map/ppermute | solution.py:23
  28.2 1.5 %collective-permute-start.6 = (bf16[192,1024]{1,0:T(8,128)(2,1)S(1)}, bf16[192,1024]{1,0:T(8,128)(2,1)S(1)}, u32[]{:S(2)}, u32[]{:S(2)}) collective-permute-start(bf16[192,1024]{1,0:T(8,128)(2,1)S(1)} %bitcast.46), channel_id=1, source_target_pairs={{0,6},{2,0},{4,2},{6,4},{1,7},{3,1},{5,3},{7,5},{8,14},{10,8},{12,... | collective-permute-start | bytes 1179656 | tf_op jit(solution)/shard_map/ppermute | solution.py:23
  29.7 4.1 %collective-permute-start.3 = (bf16[192,1024]{1,0:T(8,128)(2,1)S(1)}, bf16[192,1024]{1,0:T(8,128)(2,1)S(1)}, u32[]{:S(2)}, u32[]{:S(2)}) collective-permute-start(bf16[192,1024]{1,0:T(8,128)(2,1)S(1)} %bitcast.47), channel_id=1, source_target_pairs={{0,1},{1,0},{2,3},{3,2},{4,5},{5,4},{6,7},{7,6},{8,9},{9,8},{10,11... | collective-permute-start | bytes 1179656 | tf_op jit(solution)/shard_map/ppermute | solution.py:23
  33.9 1.3 %collective-permute-done.4 = bf16[192,1024]{1,0:T(8,128)(2,1)S(1)} collective-permute-done((bf16[192,1024]{1,0:T(8,128)(2,1)S(1)}, bf16[192,1024]{1,0:T(8,128)(2,1)S(1)}, u32[]{:S(2)}, u32[]{:S(2)}) %collective-permute-start.4) | collective-permute-done | bytes 393248 | tf_op jit(solution)/shard_map/ppermute | solution.py:23
  35.3 2.7 %collective-permute-start.9 = (bf16[96,1024]{1,0:T(8,128)(2,1)S(1)}, bf16[96,1024]{1,0:T(8,128)(2,1)S(1)}, u32[]{:S(2)}, u32[]{:S(2)}) collective-permute-start(bf16[96,1024]{1,0:T(8,128)(2,1)S(1)} %slice.41), channel_id=1, source_target_pairs={{0,6},{2,0},{4,2},{6,4},{1,7},{3,1},{5,3},{7,5},{8,14},{10,8},{12,... | collective-permute-start | bytes 589832 | tf_op jit(solution)/shard_map/ppermute | solution.py:23
  38.2 5.3 %collective-permute-start.5 = (bf16[192,1024]{1,0:T(8,128)(2,1)S(1)}, bf16[192,1024]{1,0:T(8,128)(2,1)S(1)}, u32[]{:S(2)}, u32[]{:S(2)}) collective-permute-start(bf16[192,1024]{1,0:T(8,128)(2,1)S(1)} %collective-permute-done.4), channel_id=1, source_target_pairs={{0,1},{1,0},{2,3},{3,2},{4,5},{5,4},{6,7},{7,6},{8,9},{9,8},{10,11... | collective-permute-start | bytes 1179656 | tf_op jit(solution)/shard_map/ppermute | solution.py:23
  43.5 7.0 %score.3 = f32[2,384]{1,0:T(2,128)S(1)} custom-call(bf16[384,1024]{1,0:T(8,128)(2,1)S(1)} %pad_maximum_fusion.1.queries, bf16[4096,1024]{1,0:T(8,128)(2,1)} %candidates.5, s32[1,384]{1,0:T(1,128)S(1)} %get-tuple-element.52.targets), custom_call_target="tpu_custom_call" | custom-call | flops 3221225472 | bytes 9175040 | tf_op jit(solution)/shard_map/score/pallas_call | solution.py:86
  50.7 0.8 collective-permute-start.10
  51.5 0.8 collective-permute-done.7
  52.4 0.1 pad_maximum_fusion.queries
  52.6 7.6 %score.4 = f32[2,768]{1,0:T(2,128)S(1)} custom-call(bf16[768,1024]{1,0:T(8,128)(2,1)S(1)} %pad_maximum_fusion.queries, bf16[4096,1024]{1,0:T(8,128)(2,1)S(1)} %bitcast.44, s32[1,768]{1,0:T(1,128)S(1)} %pad_add_fusion.targets), custom_call_target="tpu_custom_call" | custom-call | flops 6442450944 | bytes 9961472 | tf_op jit(solution)/shard_map/score/pallas_call | solution.py:86
  60.3 5.0 %score.5 = f32[2,384]{1,0:T(2,128)S(1)} custom-call(bf16[384,1024]{1,0:T(8,128)(2,1)S(1)} %pad_maximum_fusion.2.queries, bf16[4096,1024]{1,0:T(8,128)(2,1)S(1)} %bitcast.44, s32[1,384]{1,0:T(1,128)S(1)} %get-tuple-element.49.targets), custom_call_target="tpu_custom_call" | custom-call | flops 3221225472 | bytes 9175040 | tf_op jit(solution)/shard_map/score/pallas_call | solution.py:86
  65.5 0.2 collective-permute-start.11
  65.7 1.0 %collective-permute-done.11 = f32[2,1536]{1,0:T(2,128)S(1)} collective-permute-done((f32[2,1536]{1,0:T(2,128)S(1)}, f32[2,1536]{1,0:T(2,128)S(1)}, u32[]{:S(2)}, u32[]{:S(2)}) %collective-permute-start.11) | collective-permute-done | bytes 12320 | tf_op jit(solution)/shard_map/ppermute | solution.py:23
  67.0 11.4 %all_to_all.15 = f32[16,2,1536]{2,1,0:T(2,128)S(1)} all-to-all(f32[16,2,1536]{2,1,0:T(2,128)S(1)} %broadcast_in_dim.55), channel_id=1, replica_groups=mesh['group'=8,'x'=4,'y'=4,'core'=2] {'x','y'}, dimensions={0} | all-to-all | bytes 393216 | tf_op jit(solution)/shard_map/all_to_all | solution.py:18
  78.4 0.2 slice_reduce_fusion.3
  78.7 10.0 %all_to_all.16 = f32[8,2,1536]{2,1,0:T(2,128)S(1)} all-to-all(f32[8,2,1536]{2,1,0:T(2,128)S(1)} %broadcast_in_dim.56), channel_id=1, replica_groups=mesh['group'=8,'x'=4,'y'=4,'core'=2] {'group'}, dimensions={0} | all-to-all | bytes 196608 | tf_op jit(solution)/shard_map/all_to_all | solution.py:18
  88.8 0.1 slice_reduce_fusion.2
  88.9 0.6 fusion.8
  89.5 0.1 sub.47
  89.8 0.8 reshape.69
  (58 shorter events, 1.4 us)
Async XLA Ops:
  2.0 16.8 %all-to-all-start = ((bf16[8,6,1024]{2,1,0:T(8,128)(2,1)}), bf16[8,6,1024]{2,1,0:T(8,128)(2,1)S(1)}, u32[]{:S(2)}, u32[]{:S(2)}) async-start(bf16[8,6,1024]{2,1,0:T(8,128)(2,1)} %broadcast_in_dim.45), calls=%async_computation | async-start | bytes 262144 | tf_op jit(solution)/shard_map/all_to_all | solution.py:18
  18.8 4.8 %collective-permute-start = (bf16[48,1024]{1,0:T(8,128)(2,1)S(1)}, bf16[48,1024]{1,0:T(8,128)(2,1)S(1)}, u32[]{:S(2)}, u32[]{:S(2)}) collective-permute-start(bf16[48,1024]{1,0:T(8,128)(2,1)S(1)} %reshape.64), channel_id=1, source_target_pairs={{0,8},{8,16},{16,24},{24,0},{1,9},{9,17},{17,25},{25,1},{2,10},{10... | collective-permute-start | bytes 294920 | tf_op jit(solution)/shard_map/ppermute | solution.py:23
  20.1 3.5 %collective-permute-start.1 = (bf16[48,1024]{1,0:T(8,128)(2,1)S(1)}, bf16[48,1024]{1,0:T(8,128)(2,1)S(1)}, u32[]{:S(2)}, u32[]{:S(2)}) collective-permute-start(bf16[48,1024]{1,0:T(8,128)(2,1)S(1)} %reshape.64), channel_id=1, source_target_pairs={{0,24},{8,0},{16,8},{24,16},{1,25},{9,1},{17,9},{25,17},{2,26},{10... | collective-permute-start | bytes 294920 | tf_op jit(solution)/shard_map/ppermute | solution.py:23
  21.5 5.3 %collective-permute-start.2 = (bf16[48,1024]{1,0:T(8,128)(2,1)S(1)}, bf16[48,1024]{1,0:T(8,128)(2,1)S(1)}, u32[]{:S(2)}, u32[]{:S(2)}) collective-permute-start(bf16[48,1024]{1,0:T(8,128)(2,1)S(1)} %reshape.64), channel_id=1, source_target_pairs={{0,16},{8,24},{16,0},{24,8},{1,17},{9,25},{17,1},{25,9},{2,18},{10... | collective-permute-start | bytes 294920 | tf_op jit(solution)/shard_map/ppermute | solution.py:23
  26.8 8.4 %collective-permute-start.4 = (bf16[192,1024]{1,0:T(8,128)(2,1)S(1)}, bf16[192,1024]{1,0:T(8,128)(2,1)S(1)}, u32[]{:S(2)}, u32[]{:S(2)}) collective-permute-start(bf16[192,1024]{1,0:T(8,128)(2,1)S(1)} %bitcast.45), channel_id=1, source_target_pairs={{0,2},{2,4},{4,6},{6,0},{1,3},{3,5},{5,7},{7,1},{8,10},{10,12},{12... | collective-permute-start | bytes 1179656 | tf_op jit(solution)/shard_map/ppermute | solution.py:23
  28.2 7.1 %collective-permute-start.6 = (bf16[192,1024]{1,0:T(8,128)(2,1)S(1)}, bf16[192,1024]{1,0:T(8,128)(2,1)S(1)}, u32[]{:S(2)}, u32[]{:S(2)}) collective-permute-start(bf16[192,1024]{1,0:T(8,128)(2,1)S(1)} %bitcast.46), channel_id=1, source_target_pairs={{0,6},{2,0},{4,2},{6,4},{1,7},{3,1},{5,3},{7,5},{8,14},{10,8},{12,... | collective-permute-start | bytes 1179656 | tf_op jit(solution)/shard_map/ppermute | solution.py:23
  29.7 8.3 %collective-permute-start.3 = (bf16[192,1024]{1,0:T(8,128)(2,1)S(1)}, bf16[192,1024]{1,0:T(8,128)(2,1)S(1)}, u32[]{:S(2)}, u32[]{:S(2)}) collective-permute-start(bf16[192,1024]{1,0:T(8,128)(2,1)S(1)} %bitcast.47), channel_id=1, source_target_pairs={{0,1},{1,0},{2,3},{3,2},{4,5},{5,4},{6,7},{7,6},{8,9},{9,8},{10,11... | collective-permute-start | bytes 1179656 | tf_op jit(solution)/shard_map/ppermute | solution.py:23
  35.2 15.4 %collective-permute-start.8 = (bf16[96,1024]{1,0:T(8,128)(2,1)S(1)}, bf16[96,1024]{1,0:T(8,128)(2,1)S(1)}, u32[]{:S(2)}, u32[]{:S(2)}) collective-permute-start(bf16[96,1024]{1,0:T(8,128)(2,1)S(1)} %slice.40), channel_id=1, source_target_pairs={{0,2},{2,4},{4,6},{6,0},{1,3},{3,5},{5,7},{7,1},{8,10},{10,12},{12... | collective-permute-start | bytes 589832 | tf_op jit(solution)/shard_map/ppermute | solution.py:23
  35.3 15.3 %collective-permute-start.9 = (bf16[96,1024]{1,0:T(8,128)(2,1)S(1)}, bf16[96,1024]{1,0:T(8,128)(2,1)S(1)}, u32[]{:S(2)}, u32[]{:S(2)}) collective-permute-start(bf16[96,1024]{1,0:T(8,128)(2,1)S(1)} %slice.41), channel_id=1, source_target_pairs={{0,6},{2,0},{4,2},{6,4},{1,7},{3,1},{5,3},{7,5},{8,14},{10,8},{12,... | collective-permute-start | bytes 589832 | tf_op jit(solution)/shard_map/ppermute | solution.py:23
  38.1 14.4 %slice-start = ((s8[8388608]{0:T(1024)(128)(4,1)}), s8[4194304]{0:T(1024)(128)(4,1)S(1)}, s32[]{:S(2)}) async-start(s8[8388608]{0:T(1024)(128)(4,1)} %bitcast.43), calls=%async_computation.3 | async-start | bytes 8388608
  38.2 13.2 %collective-permute-start.5 = (bf16[192,1024]{1,0:T(8,128)(2,1)S(1)}, bf16[192,1024]{1,0:T(8,128)(2,1)S(1)}, u32[]{:S(2)}, u32[]{:S(2)}) collective-permute-start(bf16[192,1024]{1,0:T(8,128)(2,1)S(1)} %collective-permute-done.4), channel_id=1, source_target_pairs={{0,1},{1,0},{2,3},{3,2},{4,5},{5,4},{6,7},{7,6},{8,9},{9,8},{10,11... | collective-permute-start | bytes 1179656 | tf_op jit(solution)/shard_map/ppermute | solution.py:23
  43.5 9.1 %slice-start.1 = ((s8[8388608]{0:T(1024)(128)(4,1)}), s8[4194304]{0:T(1024)(128)(4,1)S(1)}, s32[]{:S(2)}) async-start(s8[8388608]{0:T(1024)(128)(4,1)} %bitcast.43), calls=%async_computation.4 | async-start | bytes 8388608
  50.5 1.8 %collective-permute-start.7 = (bf16[192,1024]{1,0:T(8,128)(2,1)S(1)}, bf16[192,1024]{1,0:T(8,128)(2,1)S(1)}, u32[]{:S(2)}, u32[]{:S(2)}) collective-permute-start(bf16[192,1024]{1,0:T(8,128)(2,1)S(1)} %collective-permute-done.6), channel_id=1, source_target_pairs={{0,1},{1,0},{2,3},{3,2},{4,5},{5,4},{6,7},{7,6},{8,9},{9,8},{10,11... | collective-permute-start | bytes 1179656 | tf_op jit(solution)/shard_map/ppermute | solution.py:23
  50.7 9.5 %collective-permute-start.10 = (bf16[192,1024]{1,0:T(8,128)(2,1)S(1)}, bf16[192,1024]{1,0:T(8,128)(2,1)S(1)}, u32[]{:S(2)}, u32[]{:S(2)}) collective-permute-start(bf16[192,1024]{1,0:T(8,128)(2,1)S(1)} %constant_dynamic-update-slice_fusion), channel_id=1, source_target_pairs={{0,1},{1,0},{2,3},{3,2},{4,5},{5,4},{6,7},{7,6},{8,9},{9,8},{10,11... | collective-permute-start | bytes 1179656 | tf_op jit(solution)/shard_map/ppermute | solution.py:23
  65.5 1.3 %collective-permute-start.11 = (f32[2,1536]{1,0:T(2,128)S(1)}, f32[2,1536]{1,0:T(2,128)S(1)}, u32[]{:S(2)}, u32[]{:S(2)}) collective-permute-start(f32[2,1536]{1,0:T(2,128)S(1)} %bitcast.51), channel_id=1, source_target_pairs={{0,1},{1,0},{2,3},{3,2},{4,5},{5,4},{6,7},{7,6},{8,9},{9,8},{10,11... | collective-permute-start | bytes 36872 | tf_op jit(solution)/shard_map/ppermute | solution.py:23

commit v3 on v2

--- a/solution.py
+++ b/solution.py
@@ -117,43 +117,51 @@
     owner = 0
     for axis, size in zip(EVERY, sizes):
         owner = owner * size + at[axis]
+    base = owner * rows
 
-    local = targets - owner * rows
-    local = local.reshape(*sizes, each).transpose(2, 3, 1, 0, 4).reshape(ys, -1)
     x_place = turned("x")
     y_place = turned("y")
+    queries, base, x_place, y_place, even = lax.optimization_barrier(
+        (queries, base, x_place, y_place, at["core"] == 0)
+    )
     line = broadcast_to_peers(queries, "group").reshape(-1, width)
-    line, local, x_place, y_place, even = lax.optimization_barrier(
-        (line, local, x_place, y_place, at["core"] == 0)
+    line, targets = lax.optimization_barrier((line, targets))
+    pieces = [(k, shifted(line, "x", k)) for k in (1, xs - 1, 2)]
+    local = targets - base
+    local = local.reshape(*sizes, each).transpose(2, 3, 1, 0, 4).reshape(ys, -1)
+    order = jnp.concatenate(
+        [lax.dynamic_slice_in_dim(local, y_place[k], 1, 0) for k in (0, 1, ys - 1, 2)], axis=1
     )
-    pieces = [(k, shifted(line, "x", k)) for k in (1, xs - 1, 2)]
+    count = local.shape[1]
+    cuts = (0, count * 2 // 3, 2 * count, 2 * count + count * 2 // 3, 4 * count)
+    wanted = [order[:, start:end] for start, end in zip(cuts, cuts[1:])]
     plane = jnp.zeros((xs, *line.shape), line.dtype)
     plane = lax.dynamic_update_index_in_dim(plane, line, x_place[0], 0)
     for step, piece in pieces:
         plane = lax.dynamic_update_index_in_dim(plane, piece, x_place[step], 0)
-    plane = plane.reshape(-1, width)
-    chosen = [lax.dynamic_slice_in_dim(local, place, 1, 0) for place in y_place]
+    plane, wanted = lax.optimization_barrier((plane.reshape(-1, width), wanted))
 
     def chip(block):
         other = shifted(block, "core", 1)
         return jnp.concatenate([jnp.where(even, block, other), jnp.where(even, other, block)])
 
     near = [shifted(plane, "y", k) for k in (1, ys - 1)]
-    mine = score(chip(plane), candidates, chosen[0], True)
+    own = chip(plane)
+    mine = score(own[: cuts[1]], candidates, wanted[0], True)
     half = plane.shape[0] // 2
     far = [shifted(near[0][:half], "y", 1), shifted(near[1][half:], "y", ys - 1)]
-    beside = score(
-        jnp.concatenate([chip(block) for block in near]),
-        candidates,
-        jnp.concatenate([chosen[1], chosen[3]], axis=1),
-    )
-    last = score(chip(jnp.concatenate(far)), candidates, chosen[2])
+    near = [chip(block) for block in near]
+    block = jnp.concatenate([own[cuts[1] :], near[0]])
+    beside = score(block, candidates, wanted[1])
+    rest = score(near[1][: cuts[1]], candidates, wanted[2])
+    block = jnp.concatenate([near[1][cuts[1] :], chip(jnp.concatenate(far))])
+    last = score(block, candidates, wanted[3])
 
-    mine, beside, last = lax.optimization_barrier((mine, beside, last))
-    found = jnp.zeros((2, ys, last.shape[1]), jnp.float32)
-    parts = [(0, mine), (1, beside[:, : last.shape[1]]), (ys - 1, beside[:, last.shape[1] :]), (2, last)]
-    for step, part in parts:
-        found = lax.dynamic_update_index_in_dim(found, part, y_place[step], 1)
+    parts = lax.optimization_barrier((mine, beside, rest, last))
+    parts = jnp.concatenate(parts, axis=1).reshape(2, ys, count)
+    found = jnp.zeros_like(parts)
+    for place, step in enumerate((0, 1, ys - 1, 2)):
+        found = lax.dynamic_update_index_in_dim(found, parts[:, place], y_place[step], 1)
     partial = found.reshape(2, -1)
     partial = merge(jnp.stack([partial, shifted(partial, "core", 1)]))
     partial = merge(broadcast_to_peers(partial, ("x", "y")))

time: 93.2 us -> 91 us (0.976)
  blocking collectives: 21.4 us -> 38 us
  starting transfers between devices: 29.5 us -> 20.5 us
  waiting for transfers between devices: 13.3 us -> 4.73 us
    all_to_all x2 -> x3, blocking collectives: 21.4 us -> 38 us  [broadcast_to_peers(): return lax.all_to_all(copies, axis, split_axis=0, concat_axis=0, tiled=True)]
    all_to_all x1 -> x0, starting transfers between devices: 9 us -> none  [broadcast_to_peers(): return lax.all_to_all(copies, axis, split_axis=0, concat_axis=0, tiled=True)]
    all_to_all x1 -> x0, waiting for transfers between devices: 6.57 us -> none  [broadcast_to_peers(): return lax.all_to_all(copies, axis, split_axis=0, concat_axis=0, tiled=True)]
    ppermute x12, waiting for transfers between devices: 6.77 us -> 4.73 us  [shifted(): lax.ppermute(value, axis, [(k, (k + step) % size) for k in range(size)])]
    pallas_call x3 -> x4, Pallas kernels: 19.6 us -> 19.1 us  [score(): pl.pallas_call(functools.partial(score_kernel, tiles), out_shape=jax.Shap...]
  transfers between devices with their start and end apart: 13 -> 12, of which waited for: 6 -> 3; matrix products, arithmetic and copies ran while one was open for 2% -> 2% of each run, Pallas kernels for 16% -> 15%
where the time goes in v3:
time: 91 us; the launch traced here: 90.2 us
  blocking collectives  38 us (42%)
  starting transfers between devices  20.5 us (23%)
  Pallas kernels  19.1 us (21%)
  waiting for transfers between devices  4.73 us (5%)
  between operations  2.87 us (3%)
  local copies, waits for them, and re-layouts  2.78 us (3%)
  other arithmetic  2.27 us (2%)
    all_to_all x3, blocking collectives, broadcast_to_peers(): return lax.all_to_all(copies, axis, split_axis=0, concat_axis=0, tiled=True)  38 us
    ppermute x12, starting transfers between devices, shifted(): lax.ppermute(value, axis, [(k, (k + step) % size) for k in range(size)])  20.5 us
    pallas_call x4, Pallas kernels, score(): pl.pallas_call(functools.partial(score_kernel, tiles), out_shape=jax.Shap...  19.1 us
    ppermute x12, waiting for transfers between devices, shifted(): lax.ppermute(value, axis, [(k, (k + step) % size) for k in range(size)])  4.73 us
  transfers between devices with their start and end apart: 12, of which 3 were waited for; matrix products, arithmetic and copies ran while one was open for 2% of the time, Pallas kernels for 15%

profile of v3, /device:TPU:1, one launch (start us, length us, event | category | flops | bytes accessed | tf_op | source)
XLA Modules:
  0.0 90.2 jit_solution(8401947118229288062)
XLA Ops:
  0.7 0.7 broadcast_in_dim.38
  1.4 16.6 %all_to_all.15 = bf16[8,6,1024]{2,1,0:T(8,128)(2,1)S(1)} all-to-all(bf16[8,6,1024]{2,1,0:T(8,128)(2,1)S(1)} %broadcast_in_dim.38), channel_id=1, replica_groups=mesh['group'=8,'x'=4,'y'=4,'core'=2] {'group'}, dimensions={0} | all-to-all | bytes 196608 | tf_op jit(solution)/shard_map/all_to_all | solution.py:18
  18.0 1.3 %collective-permute-start = (bf16[48,1024]{1,0:T(8,128)(2,1)S(1)}, bf16[48,1024]{1,0:T(8,128)(2,1)S(1)}, u32[]{:S(2)}, u32[]{:S(2)}) collective-permute-start(bf16[48,1024]{1,0:T(8,128)(2,1)S(1)} %reshape.67), channel_id=1, source_target_pairs={{0,8},{8,16},{16,24},{24,0},{1,9},{9,17},{17,25},{25,1},{2,10},{10... | collective-permute-start | bytes 294920 | tf_op jit(solution)/shard_map/ppermute | solution.py:23
  19.3 1.5 %collective-permute-start.1 = (bf16[48,1024]{1,0:T(8,128)(2,1)S(1)}, bf16[48,1024]{1,0:T(8,128)(2,1)S(1)}, u32[]{:S(2)}, u32[]{:S(2)}) collective-permute-start(bf16[48,1024]{1,0:T(8,128)(2,1)S(1)} %reshape.67), channel_id=1, source_target_pairs={{0,24},{8,0},{16,8},{24,16},{1,25},{9,1},{17,9},{25,17},{2,26},{10... | collective-permute-start | bytes 294920 | tf_op jit(solution)/shard_map/ppermute | solution.py:23
  20.7 1.5 %collective-permute-start.2 = (bf16[48,1024]{1,0:T(8,128)(2,1)S(1)}, bf16[48,1024]{1,0:T(8,128)(2,1)S(1)}, u32[]{:S(2)}, u32[]{:S(2)}) collective-permute-start(bf16[48,1024]{1,0:T(8,128)(2,1)S(1)} %reshape.67), channel_id=1, source_target_pairs={{0,16},{8,24},{16,0},{24,8},{1,17},{9,25},{17,1},{25,9},{2,18},{10... | collective-permute-start | bytes 294920 | tf_op jit(solution)/shard_map/ppermute | solution.py:23
  22.3 0.7 broadcast_subtract_fusion
  23.0 0.2 reshape.69
  23.3 0.1 reshape.70
  23.6 2.4 %collective-permute-done.2 = bf16[48,1024]{1,0:T(8,128)(2,1)S(1)} collective-permute-done((bf16[48,1024]{1,0:T(8,128)(2,1)S(1)}, bf16[48,1024]{1,0:T(8,128)(2,1)S(1)}, u32[]{:S(2)}, u32[]{:S(2)}) %collective-permute-start.2) | collective-permute-done | bytes 98336 | tf_op jit(solution)/shard_map/ppermute | solution.py:23
  26.0 1.4 %collective-permute-start.4 = (bf16[192,1024]{1,0:T(8,128)(2,1)S(1)}, bf16[192,1024]{1,0:T(8,128)(2,1)S(1)}, u32[]{:S(2)}, u32[]{:S(2)}) collective-permute-start(bf16[192,1024]{1,0:T(8,128)(2,1)S(1)} %bitcast.36), channel_id=1, source_target_pairs={{0,2},{2,4},{4,6},{6,0},{1,3},{3,5},{5,7},{7,1},{8,10},{10,12},{12... | collective-permute-start | bytes 1179656 | tf_op jit(solution)/shard_map/ppermute | solution.py:23
  27.4 1.5 %collective-permute-start.6 = (bf16[192,1024]{1,0:T(8,128)(2,1)S(1)}, bf16[192,1024]{1,0:T(8,128)(2,1)S(1)}, u32[]{:S(2)}, u32[]{:S(2)}) collective-permute-start(bf16[192,1024]{1,0:T(8,128)(2,1)S(1)} %bitcast.37), channel_id=1, source_target_pairs={{0,6},{2,0},{4,2},{6,4},{1,7},{3,1},{5,3},{7,5},{8,14},{10,8},{12,... | collective-permute-start | bytes 1179656 | tf_op jit(solution)/shard_map/ppermute | solution.py:23
  28.9 4.1 %collective-permute-start.3 = (bf16[192,1024]{1,0:T(8,128)(2,1)S(1)}, bf16[192,1024]{1,0:T(8,128)(2,1)S(1)}, u32[]{:S(2)}, u32[]{:S(2)}) collective-permute-start(bf16[192,1024]{1,0:T(8,128)(2,1)S(1)} %bitcast.38), channel_id=1, source_target_pairs={{0,1},{1,0},{2,3},{3,2},{4,5},{5,4},{6,7},{7,6},{8,9},{9,8},{10,11... | collective-permute-start | bytes 1179656 | tf_op jit(solution)/shard_map/ppermute | solution.py:23
  33.0 1.3 %collective-permute-done.4 = bf16[192,1024]{1,0:T(8,128)(2,1)S(1)} collective-permute-done((bf16[192,1024]{1,0:T(8,128)(2,1)S(1)}, bf16[192,1024]{1,0:T(8,128)(2,1)S(1)}, u32[]{:S(2)}, u32[]{:S(2)}) %collective-permute-start.4) | collective-permute-done | bytes 393248 | tf_op jit(solution)/shard_map/ppermute | solution.py:23
  34.4 0.1 collective-permute-start.8
  34.5 2.7 %collective-permute-start.9 = (bf16[96,1024]{1,0:T(8,128)(2,1)S(1)}, bf16[96,1024]{1,0:T(8,128)(2,1)S(1)}, u32[]{:S(2)}, u32[]{:S(2)}) collective-permute-start(bf16[96,1024]{1,0:T(8,128)(2,1)S(1)} %slice.85), channel_id=1, source_target_pairs={{0,6},{2,0},{4,2},{6,4},{1,7},{3,1},{5,3},{7,5},{8,14},{10,8},{12,... | collective-permute-start | bytes 589832 | tf_op jit(solution)/shard_map/ppermute | solution.py:23
  37.4 5.3 %collective-permute-start.7 = (bf16[192,1024]{1,0:T(8,128)(2,1)S(1)}, bf16[192,1024]{1,0:T(8,128)(2,1)S(1)}, u32[]{:S(2)}, u32[]{:S(2)}) collective-permute-start(bf16[192,1024]{1,0:T(8,128)(2,1)S(1)} %collective-permute-done.6), channel_id=1, source_target_pairs={{0,1},{1,0},{2,3},{3,2},{4,5},{5,4},{6,7},{7,6},{8,9},{9,8},{10,11... | collective-permute-start | bytes 1179656 | tf_op jit(solution)/shard_map/ppermute | solution.py:23
  42.6 5.6 %score.4 = f32[2,256]{1,0:T(2,128)S(1)} custom-call(bf16[256,1024]{1,0:T(8,128)(2,1)S(1)} %pad_maximum_fusion.3.queries, bf16[4096,1024]{1,0:T(8,128)(2,1)} %candidates.7, s32[1,256]{1,0:T(1,128)S(1)} %get-tuple-element.38.targets), custom_call_target="tpu_custom_call" | custom-call | flops 2147483648 | bytes 8912896 | tf_op jit(solution)/shard_map/score/pallas_call | solution.py:86
  48.3 0.2 collective-permute-start.5
  48.6 0.6 collective-permute-start.10
  49.3 2.8 %score.6 = f32[2,256]{1,0:T(2,128)S(1)} custom-call(bf16[256,1024]{1,0:T(8,128)(2,1)S(1)} %pad_maximum_fusion.2.queries, bf16[4096,1024]{1,0:T(8,128)(2,1)S(1)} %bitcast.35, s32[1,256]{1,0:T(1,128)S(1)} %get-tuple-element.40.targets), custom_call_target="tpu_custom_call" | custom-call | flops 2147483648 | bytes 8912896 | tf_op jit(solution)/shard_map/score/pallas_call | solution.py:86
  52.3 5.4 %score.5 = f32[2,512]{1,0:T(2,128)S(1)} custom-call(bf16[512,1024]{1,0:T(8,128)(2,1)S(1)} %pad_maximum_fusion.queries, bf16[4096,1024]{1,0:T(8,128)(2,1)S(1)} %bitcast.35, s32[1,512]{1,0:T(1,128)S(1)} %get-tuple-element.39.targets), custom_call_target="tpu_custom_call" | custom-call | flops 4294967296 | bytes 9437184 | tf_op jit(solution)/shard_map/score/pallas_call | solution.py:86
  57.8 5.4 %score.7 = f32[2,512]{1,0:T(2,128)S(1)} custom-call(bf16[512,1024]{1,0:T(8,128)(2,1)S(1)} %pad_maximum_fusion.1.queries, bf16[4096,1024]{1,0:T(8,128)(2,1)S(1)} %bitcast.35, s32[1,512]{1,0:T(1,128)S(1)} %get-tuple-element.41.targets), custom_call_target="tpu_custom_call" | custom-call | flops 4294967296 | bytes 9437184 | tf_op jit(solution)/shard_map/score/pallas_call | solution.py:86
  63.4 0.2 collective-permute-start.11
  63.6 1.0 %collective-permute-done.11 = f32[2,1536]{1,0:T(2,128)S(1)} collective-permute-done((f32[2,1536]{1,0:T(2,128)S(1)}, f32[2,1536]{1,0:T(2,128)S(1)}, u32[]{:S(2)}, u32[]{:S(2)}) %collective-permute-start.11) | collective-permute-done | bytes 12320 | tf_op jit(solution)/shard_map/ppermute | solution.py:23
  64.8 11.4 %all_to_all.16 = f32[16,2,1536]{2,1,0:T(2,128)S(1)} all-to-all(f32[16,2,1536]{2,1,0:T(2,128)S(1)} %broadcast_in_dim.43), channel_id=1, replica_groups=mesh['group'=8,'x'=4,'y'=4,'core'=2] {'x','y'}, dimensions={0} | all-to-all | bytes 393216 | tf_op jit(solution)/shard_map/all_to_all | solution.py:18
  76.3 0.2 slice_reduce_fusion.3
  76.6 10.0 %all_to_all.17 = f32[8,2,1536]{2,1,0:T(2,128)S(1)} all-to-all(f32[8,2,1536]{2,1,0:T(2,128)S(1)} %broadcast_in_dim.44), channel_id=1, replica_groups=mesh['group'=8,'x'=4,'y'=4,'core'=2] {'group'}, dimensions={0} | all-to-all | bytes 196608 | tf_op jit(solution)/shard_map/all_to_all | solution.py:18
  86.7 0.1 slice_reduce_fusion.2
  86.8 0.6 fusion.8
  87.4 0.1 sub.47
  87.6 0.1 copy.14
  87.7 0.8 reshape.73
  (62 shorter events, 1.3 us)
Async XLA Ops:
  18.0 5.6 %collective-permute-start = (bf16[48,1024]{1,0:T(8,128)(2,1)S(1)}, bf16[48,1024]{1,0:T(8,128)(2,1)S(1)}, u32[]{:S(2)}, u32[]{:S(2)}) collective-permute-start(bf16[48,1024]{1,0:T(8,128)(2,1)S(1)} %reshape.67), channel_id=1, source_target_pairs={{0,8},{8,16},{16,24},{24,0},{1,9},{9,17},{17,25},{25,1},{2,10},{10... | collective-permute-start | bytes 294920 | tf_op jit(solution)/shard_map/ppermute | solution.py:23
  19.3 4.3 %collective-permute-start.1 = (bf16[48,1024]{1,0:T(8,128)(2,1)S(1)}, bf16[48,1024]{1,0:T(8,128)(2,1)S(1)}, u32[]{:S(2)}, u32[]{:S(2)}) collective-permute-start(bf16[48,1024]{1,0:T(8,128)(2,1)S(1)} %reshape.67), channel_id=1, source_target_pairs={{0,24},{8,0},{16,8},{24,16},{1,25},{9,1},{17,9},{25,17},{2,26},{10... | collective-permute-start | bytes 294920 | tf_op jit(solution)/shard_map/ppermute | solution.py:23
  20.7 5.3 %collective-permute-start.2 = (bf16[48,1024]{1,0:T(8,128)(2,1)S(1)}, bf16[48,1024]{1,0:T(8,128)(2,1)S(1)}, u32[]{:S(2)}, u32[]{:S(2)}) collective-permute-start(bf16[48,1024]{1,0:T(8,128)(2,1)S(1)} %reshape.67), channel_id=1, source_target_pairs={{0,16},{8,24},{16,0},{24,8},{1,17},{9,25},{17,1},{25,9},{2,18},{10... | collective-permute-start | bytes 294920 | tf_op jit(solution)/shard_map/ppermute | solution.py:23
  26.0 8.4 %collective-permute-start.4 = (bf16[192,1024]{1,0:T(8,128)(2,1)S(1)}, bf16[192,1024]{1,0:T(8,128)(2,1)S(1)}, u32[]{:S(2)}, u32[]{:S(2)}) collective-permute-start(bf16[192,1024]{1,0:T(8,128)(2,1)S(1)} %bitcast.36), channel_id=1, source_target_pairs={{0,2},{2,4},{4,6},{6,0},{1,3},{3,5},{5,7},{7,1},{8,10},{10,12},{12... | collective-permute-start | bytes 1179656 | tf_op jit(solution)/shard_map/ppermute | solution.py:23
  27.4 7.1 %collective-permute-start.6 = (bf16[192,1024]{1,0:T(8,128)(2,1)S(1)}, bf16[192,1024]{1,0:T(8,128)(2,1)S(1)}, u32[]{:S(2)}, u32[]{:S(2)}) collective-permute-start(bf16[192,1024]{1,0:T(8,128)(2,1)S(1)} %bitcast.37), channel_id=1, source_target_pairs={{0,6},{2,0},{4,2},{6,4},{1,7},{3,1},{5,3},{7,5},{8,14},{10,8},{12,... | collective-permute-start | bytes 1179656 | tf_op jit(solution)/shard_map/ppermute | solution.py:23
  28.9 8.3 %collective-permute-start.3 = (bf16[192,1024]{1,0:T(8,128)(2,1)S(1)}, bf16[192,1024]{1,0:T(8,128)(2,1)S(1)}, u32[]{:S(2)}, u32[]{:S(2)}) collective-permute-start(bf16[192,1024]{1,0:T(8,128)(2,1)S(1)} %bitcast.38), channel_id=1, source_target_pairs={{0,1},{1,0},{2,3},{3,2},{4,5},{5,4},{6,7},{7,6},{8,9},{9,8},{10,11... | collective-permute-start | bytes 1179656 | tf_op jit(solution)/shard_map/ppermute | solution.py:23
  34.4 14.1 %collective-permute-start.8 = (bf16[96,1024]{1,0:T(8,128)(2,1)S(1)}, bf16[96,1024]{1,0:T(8,128)(2,1)S(1)}, u32[]{:S(2)}, u32[]{:S(2)}) collective-permute-start(bf16[96,1024]{1,0:T(8,128)(2,1)S(1)} %slice.84), channel_id=1, source_target_pairs={{0,2},{2,4},{4,6},{6,0},{1,3},{3,5},{5,7},{7,1},{8,10},{10,12},{12... | collective-permute-start | bytes 589832 | tf_op jit(solution)/shard_map/ppermute | solution.py:23
  34.5 14.0 %collective-permute-start.9 = (bf16[96,1024]{1,0:T(8,128)(2,1)S(1)}, bf16[96,1024]{1,0:T(8,128)(2,1)S(1)}, u32[]{:S(2)}, u32[]{:S(2)}) collective-permute-start(bf16[96,1024]{1,0:T(8,128)(2,1)S(1)} %slice.85), channel_id=1, source_target_pairs={{0,6},{2,0},{4,2},{6,4},{1,7},{3,1},{5,3},{7,5},{8,14},{10,8},{12,... | collective-permute-start | bytes 589832 | tf_op jit(solution)/shard_map/ppermute | solution.py:23
  37.2 12.1 %slice-start = ((s8[8388608]{0:T(1024)(128)(4,1)}), s8[4194304]{0:T(1024)(128)(4,1)S(1)}, s32[]{:S(2)}) async-start(s8[8388608]{0:T(1024)(128)(4,1)} %bitcast.34), calls=%async_computation.3 | async-start | bytes 8388608
  37.3 12.0 %slice-start.1 = ((s8[8388608]{0:T(1024)(128)(4,1)}), s8[4194304]{0:T(1024)(128)(4,1)S(1)}, s32[]{:S(2)}) async-start(s8[8388608]{0:T(1024)(128)(4,1)} %bitcast.34), calls=%async_computation.4 | async-start | bytes 8388608
  37.4 11.8 %collective-permute-start.7 = (bf16[192,1024]{1,0:T(8,128)(2,1)S(1)}, bf16[192,1024]{1,0:T(8,128)(2,1)S(1)}, u32[]{:S(2)}, u32[]{:S(2)}) collective-permute-start(bf16[192,1024]{1,0:T(8,128)(2,1)S(1)} %collective-permute-done.6), channel_id=1, source_target_pairs={{0,1},{1,0},{2,3},{3,2},{4,5},{5,4},{6,7},{7,6},{8,9},{9,8},{10,11... | collective-permute-start | bytes 1179656 | tf_op jit(solution)/shard_map/ppermute | solution.py:23
  48.3 3.9 %collective-permute-start.5 = (bf16[192,1024]{1,0:T(8,128)(2,1)S(1)}, bf16[192,1024]{1,0:T(8,128)(2,1)S(1)}, u32[]{:S(2)}, u32[]{:S(2)}) collective-permute-start(bf16[192,1024]{1,0:T(8,128)(2,1)S(1)} %collective-permute-done.4), channel_id=1, source_target_pairs={{0,1},{1,0},{2,3},{3,2},{4,5},{5,4},{6,7},{7,6},{8,9},{9,8},{10,11... | collective-permute-start | bytes 1179656 | tf_op jit(solution)/shard_map/ppermute | solution.py:23
  48.6 9.1 %collective-permute-start.10 = (bf16[192,1024]{1,0:T(8,128)(2,1)S(1)}, bf16[192,1024]{1,0:T(8,128)(2,1)S(1)}, u32[]{:S(2)}, u32[]{:S(2)}) collective-permute-start(bf16[192,1024]{1,0:T(8,128)(2,1)S(1)} %constant_dynamic-update-slice_fusion), channel_id=1, source_target_pairs={{0,1},{1,0},{2,3},{3,2},{4,5},{5,4},{6,7},{7,6},{8,9},{9,8},{10,11... | collective-permute-start | bytes 1179656 | tf_op jit(solution)/shard_map/ppermute | solution.py:23
  63.4 1.3 %collective-permute-start.11 = (f32[2,1536]{1,0:T(2,128)S(1)}, f32[2,1536]{1,0:T(2,128)S(1)}, u32[]{:S(2)}, u32[]{:S(2)}) collective-permute-start(f32[2,1536]{1,0:T(2,128)S(1)} %bitcast.43), channel_id=1, source_target_pairs={{0,1},{1,0},{2,3},{3,2},{4,5},{5,4},{6,7},{7,6},{8,9},{9,8},{10,11... | collective-permute-start | bytes 36872 | tf_op jit(solution)/shard_map/ppermute | solution.py:23

commit v4 on v3

--- a/solution.py
+++ b/solution.py
@@ -21,6 +21,16 @@
 def shifted(value, axis, step):
     size = lax.axis_size(axis)
     return lax.ppermute(value, axis, [(k, (k + step) % size) for k in range(size)])
+
+
+def forwarded(value):
+    ys, cores = lax.axis_size("y"), lax.axis_size("core")
+    pairs = [
+        (y * cores + core, (y + (1, ys - 1)[core]) % ys * cores + core)
+        for y in range(ys)
+        for core in range(cores)
+    ]
+    return lax.ppermute(value, ("y", "core"), pairs)
 
 
 def turned(axis):
@@ -101,6 +111,48 @@
     )(queries, candidates, targets)
 
 
+def pick_kernel(first_wanted, first, second, out):
+    @pl.when(first_wanted[0] == 1)
+    def _():
+        out[...] = first[...]
+
+    @pl.when(first_wanted[0] == 0)
+    def _():
+        out[...] = second[...]
+
+
+def picked_block(first_wanted, first, second):
+    vmem = pl.BlockSpec(memory_space=pltpu.VMEM)
+    return pl.pallas_call(
+        pick_kernel,
+        out_shape=jax.ShapeDtypeStruct(first.shape, first.dtype),
+        in_specs=[pl.BlockSpec(memory_space=pltpu.SMEM), vmem, vmem],
+        out_specs=vmem,
+        compiler_params=pltpu.CompilerParams(vmem_limit_bytes=4 * 2**20),
+        cost_estimate=pl.CostEstimate(
+            flops=10**6, bytes_accessed=4 * first.size, transcendentals=0
+        ),
+        name="pick",
+    )(first_wanted, first, second)
+
+
+def prep_kernel(value, out):
+    out[...] = value[...]
+
+
+def prepared(value):
+    vmem = pl.BlockSpec(memory_space=pltpu.VMEM)
+    return pl.pallas_call(
+        prep_kernel,
+        out_shape=jax.ShapeDtypeStruct(value.shape, value.dtype),
+        in_specs=[vmem],
+        out_specs=vmem,
+        compiler_params=pltpu.CompilerParams(vmem_limit_bytes=2**20),
+        cost_estimate=pl.CostEstimate(flops=2 * 10**10, bytes_accessed=4096, transcendentals=0),
+        name="prep",
+    )(value)
+
+
 def merge(parts):
     lse, picked = parts[:, 0], parts[:, 1]
     top = jnp.max(lse, axis=0)
@@ -121,8 +173,9 @@
 
     x_place = turned("x")
     y_place = turned("y")
-    queries, base, x_place, y_place, even = lax.optimization_barrier(
-        (queries, base, x_place, y_place, at["core"] == 0)
+    first_wanted = (at["core"] == 0).astype(jnp.int32).reshape(1)
+    queries, base, x_place, y_place, even, first_wanted = lax.optimization_barrier(
+        (queries, base, x_place, y_place, at["core"] == 0, first_wanted)
     )
     line = broadcast_to_peers(queries, "group").reshape(-1, width)
     line, targets = lax.optimization_barrier((line, targets))
@@ -147,14 +200,13 @@
 
     near = [shifted(plane, "y", k) for k in (1, ys - 1)]
     own = chip(plane)
-    mine = score(own[: cuts[1]], candidates, wanted[0], True)
-    half = plane.shape[0] // 2
-    far = [shifted(near[0][:half], "y", 1), shifted(near[1][half:], "y", ys - 1)]
+    mine = score(own[: cuts[1]], candidates, prepared(wanted[0]))
+    far = forwarded(picked_block(first_wanted, *near))
     near = [chip(block) for block in near]
     block = jnp.concatenate([own[cuts[1] :], near[0]])
     beside = score(block, candidates, wanted[1])
     rest = score(near[1][: cuts[1]], candidates, wanted[2])
-    block = jnp.concatenate([near[1][cuts[1] :], chip(jnp.concatenate(far))])
+    block = jnp.concatenate([near[1][cuts[1] :], chip(far)])
     last = score(block, candidates, wanted[3])
 
     parts = lax.optimization_barrier((mine, beside, rest, last))

time: 91 us -> 90.1 us (level)
  waiting for transfers between devices: 4.73 us -> 12.7 us
  starting transfers between devices: 20.5 us -> 14.8 us
  Pallas kernels: 19.1 us -> 16.4 us
    ppermute x12 -> x10, waiting for transfers between devices: 4.73 us -> 12.7 us  [shifted(): lax.ppermute(value, axis, [(k, (k + step) % size) for k in range(size)])]
    ppermute x12 -> x10, starting transfers between devices: 20.5 us -> 13.3 us  [shifted(): lax.ppermute(value, axis, [(k, (k + step) % size) for k in range(size)])]
    pallas_call x4, Pallas kernels: 19.1 us -> 16.4 us  [score(): pl.pallas_call(functools.partial(score_kernel, tiles), out_shape=jax.Shap...]
    ppermute x0 -> x1, starting transfers between devices: none -> 1.54 us  [forwarded(): return lax.ppermute(value, ('y', 'core'), pairs)]
  transfers between devices with their start and end apart: 12 -> 11, of which waited for: 3 -> 3; matrix products, arithmetic and copies ran while one was open for 2% -> 2% of each run, Pallas kernels for 15% -> 12%
where the time goes in v4:
time: 90.1 us; the launch traced here: 89.4 us
  blocking collectives  37.6 us (42%)
  Pallas kernels  16.4 us (18%)
  starting transfers between devices  14.8 us (16%)
  waiting for transfers between devices  12.7 us (14%)
  between operations  2.85 us (3%)
  local copies, waits for them, and re-layouts  2.73 us (3%)
  other arithmetic  2.32 us (3%)
    all_to_all x3, blocking collectives, broadcast_to_peers(): return lax.all_to_all(copies, axis, split_axis=0, concat_axis=0, tiled=True)  37.6 us
    pallas_call x4, Pallas kernels, score(): pl.pallas_call(functools.partial(score_kernel, tiles), out_shape=jax.Shap...  16.4 us
    ppermute x10, starting transfers between devices, shifted(): lax.ppermute(value, axis, [(k, (k + step) % size) for k in range(size)])  13.3 us
    ppermute x10, waiting for transfers between devices, shifted(): lax.ppermute(value, axis, [(k, (k + step) % size) for k in range(size)])  12.7 us
  transfers between devices with their start and end apart: 11, of which 3 were waited for; matrix products, arithmetic and copies ran while one was open for 2% of the time, Pallas kernels for 12%

profile of v4, /device:TPU:1, one launch (start us, length us, event | category | flops | bytes accessed | tf_op | source)
XLA Modules:
  0.0 89.4 jit_solution(17163613975088535884)
XLA Ops:
  0.7 0.7 broadcast_in_dim.38
  1.4 16.6 %all_to_all.15 = bf16[8,6,1024]{2,1,0:T(8,128)(2,1)S(1)} all-to-all(bf16[8,6,1024]{2,1,0:T(8,128)(2,1)S(1)} %broadcast_in_dim.38), channel_id=1, replica_groups=mesh['group'=8,'x'=4,'y'=4,'core'=2] {'group'}, dimensions={0} | all-to-all | bytes 196608 | tf_op jit(solution)/shard_map/all_to_all | solution.py:18
  18.0 1.3 %collective-permute-start = (bf16[48,1024]{1,0:T(8,128)(2,1)S(1)}, bf16[48,1024]{1,0:T(8,128)(2,1)S(1)}, u32[]{:S(2)}, u32[]{:S(2)}) collective-permute-start(bf16[48,1024]{1,0:T(8,128)(2,1)S(1)} %reshape.75), channel_id=1, source_target_pairs={{0,8},{8,16},{16,24},{24,0},{1,9},{9,17},{17,25},{25,1},{2,10},{10... | collective-permute-start | bytes 294920 | tf_op jit(solution)/shard_map/ppermute | solution.py:23
  19.3 1.5 %collective-permute-start.1 = (bf16[48,1024]{1,0:T(8,128)(2,1)S(1)}, bf16[48,1024]{1,0:T(8,128)(2,1)S(1)}, u32[]{:S(2)}, u32[]{:S(2)}) collective-permute-start(bf16[48,1024]{1,0:T(8,128)(2,1)S(1)} %reshape.75), channel_id=1, source_target_pairs={{0,24},{8,0},{16,8},{24,16},{1,25},{9,1},{17,9},{25,17},{2,26},{10... | collective-permute-start | bytes 294920 | tf_op jit(solution)/shard_map/ppermute | solution.py:23
  20.7 1.5 %collective-permute-start.2 = (bf16[48,1024]{1,0:T(8,128)(2,1)S(1)}, bf16[48,1024]{1,0:T(8,128)(2,1)S(1)}, u32[]{:S(2)}, u32[]{:S(2)}) collective-permute-start(bf16[48,1024]{1,0:T(8,128)(2,1)S(1)} %reshape.75), channel_id=1, source_target_pairs={{0,16},{8,24},{16,0},{24,8},{1,17},{9,25},{17,1},{25,9},{2,18},{10... | collective-permute-start | bytes 294920 | tf_op jit(solution)/shard_map/ppermute | solution.py:23
  22.3 0.7 broadcast_subtract_fusion
  23.0 0.2 reshape.77
  23.2 0.1 copy.9
  23.3 0.1 reshape.78
  23.6 2.4 %collective-permute-done.2 = bf16[48,1024]{1,0:T(8,128)(2,1)S(1)} collective-permute-done((bf16[48,1024]{1,0:T(8,128)(2,1)S(1)}, bf16[48,1024]{1,0:T(8,128)(2,1)S(1)}, u32[]{:S(2)}, u32[]{:S(2)}) %collective-permute-start.2) | collective-permute-done | bytes 98336 | tf_op jit(solution)/shard_map/ppermute | solution.py:23
  26.0 3.8 %collective-permute-start.3 = (bf16[192,1024]{1,0:T(8,128)(2,1)S(1)}, bf16[192,1024]{1,0:T(8,128)(2,1)S(1)}, u32[]{:S(2)}, u32[]{:S(2)}) collective-permute-start(bf16[192,1024]{1,0:T(8,128)(2,1)S(1)} %bitcast.37), channel_id=1, source_target_pairs={{0,1},{1,0},{2,3},{3,2},{4,5},{5,4},{6,7},{7,6},{8,9},{9,8},{10,11... | collective-permute-start | bytes 1179656 | tf_op jit(solution)/shard_map/ppermute | solution.py:23
  29.8 1.3 %collective-permute-start.4 = (bf16[192,1024]{1,0:T(8,128)(2,1)S(1)}, bf16[192,1024]{1,0:T(8,128)(2,1)S(1)}, u32[]{:S(2)}, u32[]{:S(2)}) collective-permute-start(bf16[192,1024]{1,0:T(8,128)(2,1)S(1)} %bitcast.38), channel_id=1, source_target_pairs={{0,2},{2,4},{4,6},{6,0},{1,3},{3,5},{5,7},{7,1},{8,10},{10,12},{12... | collective-permute-start | bytes 1179656 | tf_op jit(solution)/shard_map/ppermute | solution.py:23
  31.1 1.4 %collective-permute-start.6 = (bf16[192,1024]{1,0:T(8,128)(2,1)S(1)}, bf16[192,1024]{1,0:T(8,128)(2,1)S(1)}, u32[]{:S(2)}, u32[]{:S(2)}) collective-permute-start(bf16[192,1024]{1,0:T(8,128)(2,1)S(1)} %bitcast.39), channel_id=1, source_target_pairs={{0,6},{2,0},{4,2},{6,4},{1,7},{3,1},{5,3},{7,5},{8,14},{10,8},{12,... | collective-permute-start | bytes 1179656 | tf_op jit(solution)/shard_map/ppermute | solution.py:23
  32.6 9.2 %collective-permute-done.4.first = bf16[192,1024]{1,0:T(8,128)(2,1)S(1)} collective-permute-done((bf16[192,1024]{1,0:T(8,128)(2,1)S(1)}, bf16[192,1024]{1,0:T(8,128)(2,1)S(1)}, u32[]{:S(2)}, u32[]{:S(2)}) %collective-permute-start.4) | collective-permute-done | bytes 393248 | tf_op jit(solution)/shard_map/ppermute | solution.py:23
  41.8 0.9 collective-permute-start.5
  42.8 1.5 %collective-permute-start.8 = (bf16[192,1024]{1,0:T(8,128)(2,1)S(1)}, bf16[192,1024]{1,0:T(8,128)(2,1)S(1)}, u32[]{:S(2)}, u32[]{:S(2)}) collective-permute-start(bf16[192,1024]{1,0:T(8,128)(2,1)S(1)} %pick.1), channel_id=1, source_target_pairs={{0,2},{1,7},{2,4},{3,1},{4,6},{5,3},{6,0},{7,5},{8,10},{9,15},{10,... | collective-permute-start | bytes 1179656 | tf_op jit(solution)/shard_map/ppermute | solution.py:33
  44.4 2.9 %score.4 = f32[2,256]{1,0:T(2,128)S(1)} custom-call(bf16[256,1024]{1,0:T(8,128)(2,1)S(1)} %pad_maximum_fusion.3.queries, bf16[4096,1024]{1,0:T(8,128)(2,1)S(1)} %bitcast.36, s32[1,256]{1,0:T(1,128)S(1)} %prep.1.targets), custom_call_target="tpu_custom_call" | custom-call | flops 2147483648 | bytes 8912896 | tf_op jit(solution)/shard_map/score/pallas_call | solution.py:96
  47.4 0.1 broadcast_select_fusion.3
  47.6 2.8 %score.6 = f32[2,256]{1,0:T(2,128)S(1)} custom-call(bf16[256,1024]{1,0:T(8,128)(2,1)S(1)} %pad_maximum_fusion.2.queries, bf16[4096,1024]{1,0:T(8,128)(2,1)S(1)} %bitcast.36, s32[1,256]{1,0:T(1,128)S(1)} %get-tuple-element.41.targets), custom_call_target="tpu_custom_call" | custom-call | flops 2147483648 | bytes 8912896 | tf_op jit(solution)/shard_map/score/pallas_call | solution.py:96
  50.4 1.4 %collective-permute-start.9 = (bf16[192,1024]{1,0:T(8,128)(2,1)S(1)}, bf16[192,1024]{1,0:T(8,128)(2,1)S(1)}, u32[]{:S(2)}, u32[]{:S(2)}) collective-permute-start(bf16[192,1024]{1,0:T(8,128)(2,1)S(1)} %collective-permute-done.8), channel_id=1, source_target_pairs={{0,1},{1,0},{2,3},{3,2},{4,5},{5,4},{6,7},{7,6},{8,9},{9,8},{10,11... | collective-permute-start | bytes 1179656 | tf_op jit(solution)/shard_map/ppermute | solution.py:23
  51.9 5.4 %score.5 = f32[2,512]{1,0:T(2,128)S(1)} custom-call(bf16[512,1024]{1,0:T(8,128)(2,1)S(1)} %pad_maximum_fusion.queries, bf16[4096,1024]{1,0:T(8,128)(2,1)S(1)} %bitcast.36, s32[1,512]{1,0:T(1,128)S(1)} %get-tuple-element.40.targets), custom_call_target="tpu_custom_call" | custom-call | flops 4294967296 | bytes 9437184 | tf_op jit(solution)/shard_map/score/pallas_call | solution.py:96
  57.4 5.4 %score.7 = f32[2,512]{1,0:T(2,128)S(1)} custom-call(bf16[512,1024]{1,0:T(8,128)(2,1)S(1)} %pad_maximum_fusion.1.queries, bf16[4096,1024]{1,0:T(8,128)(2,1)S(1)} %bitcast.36, s32[1,512]{1,0:T(1,128)S(1)} %get-tuple-element.43.targets), custom_call_target="tpu_custom_call" | custom-call | flops 4294967296 | bytes 9437184 | tf_op jit(solution)/shard_map/score/pallas_call | solution.py:96
  63.0 0.1 collective-permute-start.10
  63.1 1.1 %collective-permute-done.10 = f32[2,1536]{1,0:T(2,128)S(1)} collective-permute-done((f32[2,1536]{1,0:T(2,128)S(1)}, f32[2,1536]{1,0:T(2,128)S(1)}, u32[]{:S(2)}, u32[]{:S(2)}) %collective-permute-start.10) | collective-permute-done | bytes 12320 | tf_op jit(solution)/shard_map/ppermute | solution.py:23
  64.4 11.0 %all_to_all.16 = f32[16,2,1536]{2,1,0:T(2,128)S(1)} all-to-all(f32[16,2,1536]{2,1,0:T(2,128)S(1)} %broadcast_in_dim.43), channel_id=1, replica_groups=mesh['group'=8,'x'=4,'y'=4,'core'=2] {'x','y'}, dimensions={0} | all-to-all | bytes 393216 | tf_op jit(solution)/shard_map/all_to_all | solution.py:18
  75.4 0.2 slice_reduce_fusion.3
  75.8 10.0 %all_to_all.17 = f32[8,2,1536]{2,1,0:T(2,128)S(1)} all-to-all(f32[8,2,1536]{2,1,0:T(2,128)S(1)} %broadcast_in_dim.44), channel_id=1, replica_groups=mesh['group'=8,'x'=4,'y'=4,'core'=2] {'group'}, dimensions={0} | all-to-all | bytes 196608 | tf_op jit(solution)/shard_map/all_to_all | solution.py:18
  85.8 0.1 slice_reduce_fusion.2
  86.0 0.6 fusion.8
  86.6 0.1 sub.47
  86.7 0.1 copy.14
  86.8 0.8 reshape.81
  (58 shorter events, 1.2 us)
Async XLA Ops:
  18.0 5.6 %collective-permute-start = (bf16[48,1024]{1,0:T(8,128)(2,1)S(1)}, bf16[48,1024]{1,0:T(8,128)(2,1)S(1)}, u32[]{:S(2)}, u32[]{:S(2)}) collective-permute-start(bf16[48,1024]{1,0:T(8,128)(2,1)S(1)} %reshape.75), channel_id=1, source_target_pairs={{0,8},{8,16},{16,24},{24,0},{1,9},{9,17},{17,25},{25,1},{2,10},{10... | collective-permute-start | bytes 294920 | tf_op jit(solution)/shard_map/ppermute | solution.py:23
  19.3 4.3 %collective-permute-start.1 = (bf16[48,1024]{1,0:T(8,128)(2,1)S(1)}, bf16[48,1024]{1,0:T(8,128)(2,1)S(1)}, u32[]{:S(2)}, u32[]{:S(2)}) collective-permute-start(bf16[48,1024]{1,0:T(8,128)(2,1)S(1)} %reshape.75), channel_id=1, source_target_pairs={{0,24},{8,0},{16,8},{24,16},{1,25},{9,1},{17,9},{25,17},{2,26},{10... | collective-permute-start | bytes 294920 | tf_op jit(solution)/shard_map/ppermute | solution.py:23
  20.7 5.3 %collective-permute-start.2 = (bf16[48,1024]{1,0:T(8,128)(2,1)S(1)}, bf16[48,1024]{1,0:T(8,128)(2,1)S(1)}, u32[]{:S(2)}, u32[]{:S(2)}) collective-permute-start(bf16[48,1024]{1,0:T(8,128)(2,1)S(1)} %reshape.75), channel_id=1, source_target_pairs={{0,16},{8,24},{16,0},{24,8},{1,17},{9,25},{17,1},{25,9},{2,18},{10... | collective-permute-start | bytes 294920 | tf_op jit(solution)/shard_map/ppermute | solution.py:23
  26.0 18.4 %slice-start = ((s8[8388608]{0:T(1024)(128)(4,1)}), s8[4194304]{0:T(1024)(128)(4,1)S(1)}, s32[]{:S(2)}) async-start(s8[8388608]{0:T(1024)(128)(4,1)} %bitcast.35), calls=%async_computation.3 | async-start | bytes 8388608
  26.0 18.4 %slice-start.1 = ((s8[8388608]{0:T(1024)(128)(4,1)}), s8[4194304]{0:T(1024)(128)(4,1)S(1)}, s32[]{:S(2)}) async-start(s8[8388608]{0:T(1024)(128)(4,1)} %bitcast.35), calls=%async_computation.4 | async-start | bytes 8388608
  26.0 16.6 %collective-permute-start.3 = (bf16[192,1024]{1,0:T(8,128)(2,1)S(1)}, bf16[192,1024]{1,0:T(8,128)(2,1)S(1)}, u32[]{:S(2)}, u32[]{:S(2)}) collective-permute-start(bf16[192,1024]{1,0:T(8,128)(2,1)S(1)} %bitcast.37), channel_id=1, source_target_pairs={{0,1},{1,0},{2,3},{3,2},{4,5},{5,4},{6,7},{7,6},{8,9},{9,8},{10,11... | collective-permute-start | bytes 1179656 | tf_op jit(solution)/shard_map/ppermute | solution.py:23
  29.8 11.9 %collective-permute-start.4 = (bf16[192,1024]{1,0:T(8,128)(2,1)S(1)}, bf16[192,1024]{1,0:T(8,128)(2,1)S(1)}, u32[]{:S(2)}, u32[]{:S(2)}) collective-permute-start(bf16[192,1024]{1,0:T(8,128)(2,1)S(1)} %bitcast.38), channel_id=1, source_target_pairs={{0,2},{2,4},{4,6},{6,0},{1,3},{3,5},{5,7},{7,1},{8,10},{10,12},{12... | collective-permute-start | bytes 1179656 | tf_op jit(solution)/shard_map/ppermute | solution.py:23
  31.1 11.6 %collective-permute-start.6 = (bf16[192,1024]{1,0:T(8,128)(2,1)S(1)}, bf16[192,1024]{1,0:T(8,128)(2,1)S(1)}, u32[]{:S(2)}, u32[]{:S(2)}) collective-permute-start(bf16[192,1024]{1,0:T(8,128)(2,1)S(1)} %bitcast.39), channel_id=1, source_target_pairs={{0,6},{2,0},{4,2},{6,4},{1,7},{3,1},{5,3},{7,5},{8,14},{10,8},{12,... | collective-permute-start | bytes 1179656 | tf_op jit(solution)/shard_map/ppermute | solution.py:23
  41.8 5.5 %collective-permute-start.5 = (bf16[192,1024]{1,0:T(8,128)(2,1)S(1)}, bf16[192,1024]{1,0:T(8,128)(2,1)S(1)}, u32[]{:S(2)}, u32[]{:S(2)}) collective-permute-start(bf16[192,1024]{1,0:T(8,128)(2,1)S(1)} %collective-permute-done.4.first), channel_id=1, source_target_pairs={{0,1},{1,0},{2,3},{3,2},{4,5},{5,4},{6,7},{7,6},{8,9},{9,8},{10,11... | collective-permute-start | bytes 1179656 | tf_op jit(solution)/shard_map/ppermute | solution.py:23
  42.8 7.6 %collective-permute-start.8 = (bf16[192,1024]{1,0:T(8,128)(2,1)S(1)}, bf16[192,1024]{1,0:T(8,128)(2,1)S(1)}, u32[]{:S(2)}, u32[]{:S(2)}) collective-permute-start(bf16[192,1024]{1,0:T(8,128)(2,1)S(1)} %pick.1), channel_id=1, source_target_pairs={{0,2},{1,7},{2,4},{3,1},{4,6},{5,3},{6,0},{7,5},{8,10},{9,15},{10,... | collective-permute-start | bytes 1179656 | tf_op jit(solution)/shard_map/ppermute | solution.py:33
  44.3 3.0 %collective-permute-start.7 = (bf16[192,1024]{1,0:T(8,128)(2,1)S(1)}, bf16[192,1024]{1,0:T(8,128)(2,1)S(1)}, u32[]{:S(2)}, u32[]{:S(2)}) collective-permute-start(bf16[192,1024]{1,0:T(8,128)(2,1)S(1)} %collective-permute-done.6.second), channel_id=1, source_target_pairs={{0,1},{1,0},{2,3},{3,2},{4,5},{5,4},{6,7},{7,6},{8,9},{9,8},{10,11... | collective-permute-start | bytes 1179656 | tf_op jit(solution)/shard_map/ppermute | solution.py:23
  50.4 6.8 %collective-permute-start.9 = (bf16[192,1024]{1,0:T(8,128)(2,1)S(1)}, bf16[192,1024]{1,0:T(8,128)(2,1)S(1)}, u32[]{:S(2)}, u32[]{:S(2)}) collective-permute-start(bf16[192,1024]{1,0:T(8,128)(2,1)S(1)} %collective-permute-done.8), channel_id=1, source_target_pairs={{0,1},{1,0},{2,3},{3,2},{4,5},{5,4},{6,7},{7,6},{8,9},{9,8},{10,11... | collective-permute-start | bytes 1179656 | tf_op jit(solution)/shard_map/ppermute | solution.py:23
  63.0 1.3 %collective-permute-start.10 = (f32[2,1536]{1,0:T(2,128)S(1)}, f32[2,1536]{1,0:T(2,128)S(1)}, u32[]{:S(2)}, u32[]{:S(2)}) collective-permute-start(f32[2,1536]{1,0:T(2,128)S(1)} %bitcast.44), channel_id=1, source_target_pairs={{0,1},{1,0},{2,3},{3,2},{4,5},{5,4},{6,7},{7,6},{8,9},{9,8},{10,11... | collective-permute-start | bytes 36872 | tf_op jit(solution)/shard_map/ppermute | solution.py:23

commit v5 on v4

--- a/solution.py
+++ b/solution.py
@@ -39,26 +39,15 @@
     return [lax.rem(at + jnp.uint32(size - k), jnp.uint32(size)) for k in range(size)]
 
 
-def score_kernel(tiles, queries, candidates, targets, out, scores, *stream):
+def score_kernel(tiles, queries, candidates, targets, out, scores):
     count = queries.shape[0]
     starts = [sum(tiles[:k]) for k in range(len(tiles))]
     places = [pl.ds(start, tile) for start, tile in zip(starts, tiles)]
     local = targets[...] - lax.broadcasted_iota(jnp.int32, (8, count), 0)
-    source, copies = candidates, {}
-    if stream:
-        source, sems = stream
-        cuts = [0, starts[1], starts[len(tiles) // 2], candidates.shape[0]]
-        for k, (start, end) in enumerate(zip(cuts, cuts[1:])):
-            part = pl.ds(start, end - start)
-            copy = pltpu.make_async_copy(candidates.at[part], source.at[part], sems.at[k])
-            copy.start()
-            copies[starts.index(start)] = copy
 
     def multiply(k):
-        if k in copies:
-            copies[k].wait()
         scores[k % 2, : tiles[k]] = lax.dot_general(
-            source[places[k], :],
+            candidates[places[k], :],
             queries[...],
             (((1,), (1,)), ((), ())),
             preferred_element_type=jnp.float32,
@@ -82,25 +71,22 @@
     out[1:2, :] = jnp.sum(picked, axis=0, keepdims=True)
 
 
-def score(queries, candidates, targets, streamed=False):
+def score(queries, candidates, targets):
     count, width = queries.shape
     rows = candidates.shape[0]
-    tiles = [TILE // 2] + [TILE] * (rows // TILE - 1) + [TILE // 2]
-    scratch = [pltpu.VMEM((2, TILE, count), jnp.float32)]
-    if streamed:
-        scratch += [
-            pltpu.VMEM(candidates.shape, candidates.dtype),
-            pltpu.SemaphoreType.DMA((3,)),
-        ]
+    edge = [TILE // 2] if count <= 256 else [TILE // 2, TILE + TILE // 2]
+    inner = TILE if count <= 256 else 2 * TILE
+    tiles = edge + [inner] * ((rows - 2 * sum(edge)) // inner) + edge[::-1]
+    scratch = [pltpu.VMEM((2, max(tiles), count), jnp.float32)]
     vmem = pl.BlockSpec(memory_space=pltpu.VMEM)
     return pl.pallas_call(
         functools.partial(score_kernel, tiles),
         out_shape=jax.ShapeDtypeStruct((2, count), jnp.float32),
-        in_specs=[vmem, pl.BlockSpec(memory_space=pl.ANY) if streamed else vmem, vmem],
+        in_specs=[vmem] * 3,
         out_specs=vmem,
         scratch_shapes=scratch,
         compiler_params=pltpu.CompilerParams(
-            vmem_limit_bytes=(50 if streamed else 16) * 2**20
+            vmem_limit_bytes=16 * 2**20
         ),
         cost_estimate=pl.CostEstimate(
             flops=2 * count * rows * width,
@@ -158,6 +144,30 @@
     top = jnp.max(lse, axis=0)
     lse = top + jnp.log(jnp.sum(jnp.exp(lse - top), axis=0))
     return jnp.stack([lse, jnp.sum(picked, axis=0)])
+
+
+def close_kernel(parts, losses, mean):
+    lse, picked = parts[:, 0, :], parts[:, 1, :]
+    top = jnp.max(lse, axis=0, keepdims=True)
+    total = jnp.sum(jnp.exp(lse - top), axis=0, keepdims=True)
+    result = top + jnp.log(total) - jnp.sum(picked, axis=0, keepdims=True)
+    losses[...] = result
+    mean[...] = jnp.sum(result, axis=1, keepdims=True) / result.shape[1]
+
+
+def closed(parts):
+    vmem = pl.BlockSpec(memory_space=pltpu.VMEM)
+    return pl.pallas_call(
+        close_kernel,
+        out_shape=(
+            jax.ShapeDtypeStruct((1, parts.shape[2]), jnp.float32),
+            jax.ShapeDtypeStruct((1, 1), jnp.float32),
+        ),
+        in_specs=[vmem],
+        out_specs=(vmem, vmem),
+        compiler_params=pltpu.CompilerParams(vmem_limit_bytes=4 * 2**20),
+        name="close",
+    )(parts)
 
 
 def on_device(queries, candidates, targets):
@@ -217,10 +227,9 @@
     partial = found.reshape(2, -1)
     partial = merge(jnp.stack([partial, shifted(partial, "core", 1)]))
     partial = merge(broadcast_to_peers(partial, ("x", "y")))
-    lse, picked = merge(broadcast_to_peers(partial, "group"))
-    losses = lse - picked
+    losses, mean = closed(broadcast_to_peers(partial, "group"))
     losses = losses.reshape(ys, cores, xs, groups, each).transpose(3, 2, 0, 1, 4).reshape(-1)
-    return (losses, jnp.mean(losses))
+    return (losses, mean.reshape(()))
 
 
 def solution(mesh):

time: 90.1 us -> 87.7 us (0.973)
  between operations: 2.85 us -> 1.07 us
where the time goes in v5:
time: 87.7 us; the launch traced here: 87 us
  blocking collectives  37.6 us (43%)
  Pallas kernels  16.5 us (19%)
  starting transfers between devices  14.8 us (17%)
  waiting for transfers between devices  12.7 us (14%)
  local copies, waits for them, and re-layouts  2.73 us (3%)
  other arithmetic  1.58 us (2%)
  between operations  1.07 us (1%)
    all_to_all x3, blocking collectives, broadcast_to_peers(): return lax.all_to_all(copies, axis, split_axis=0, concat_axis=0, tiled=True)  37.6 us
    pallas_call x4, Pallas kernels, score(): pl.pallas_call(functools.partial(score_kernel, tiles), out_shape=jax.Shap...  15.8 us
    ppermute x10, starting transfers between devices, shifted(): lax.ppermute(value, axis, [(k, (k + step) % size) for k in range(size)])  13.3 us
    ppermute x10, waiting for transfers between devices, shifted(): lax.ppermute(value, axis, [(k, (k + step) % size) for k in range(size)])  12.7 us
  transfers between devices with their start and end apart: 11, of which 3 were waited for; matrix products, arithmetic and copies ran while one was open for 2% of the time, Pallas kernels for 12%

profile of v5, /device:TPU:1, one launch (start us, length us, event | category | flops | bytes accessed | tf_op | source)
XLA Modules:
  0.0 87.0 jit_solution(7478068784711612594)
XLA Ops:
  0.7 0.7 broadcast_in_dim.37
  1.4 16.6 %all_to_all.15 = bf16[8,6,1024]{2,1,0:T(8,128)(2,1)S(1)} all-to-all(bf16[8,6,1024]{2,1,0:T(8,128)(2,1)S(1)} %broadcast_in_dim.37), channel_id=1, replica_groups=mesh['group'=8,'x'=4,'y'=4,'core'=2] {'group'}, dimensions={0} | all-to-all | bytes 196608 | tf_op jit(solution)/shard_map/all_to_all | solution.py:18
  18.0 1.3 %collective-permute-start = (bf16[48,1024]{1,0:T(8,128)(2,1)S(1)}, bf16[48,1024]{1,0:T(8,128)(2,1)S(1)}, u32[]{:S(2)}, u32[]{:S(2)}) collective-permute-start(bf16[48,1024]{1,0:T(8,128)(2,1)S(1)} %reshape.73), channel_id=1, source_target_pairs={{0,8},{8,16},{16,24},{24,0},{1,9},{9,17},{17,25},{25,1},{2,10},{10... | collective-permute-start | bytes 294920 | tf_op jit(solution)/shard_map/ppermute | solution.py:23
  19.3 1.5 %collective-permute-start.1 = (bf16[48,1024]{1,0:T(8,128)(2,1)S(1)}, bf16[48,1024]{1,0:T(8,128)(2,1)S(1)}, u32[]{:S(2)}, u32[]{:S(2)}) collective-permute-start(bf16[48,1024]{1,0:T(8,128)(2,1)S(1)} %reshape.73), channel_id=1, source_target_pairs={{0,24},{8,0},{16,8},{24,16},{1,25},{9,1},{17,9},{25,17},{2,26},{10... | collective-permute-start | bytes 294920 | tf_op jit(solution)/shard_map/ppermute | solution.py:23
  20.7 1.5 %collective-permute-start.2 = (bf16[48,1024]{1,0:T(8,128)(2,1)S(1)}, bf16[48,1024]{1,0:T(8,128)(2,1)S(1)}, u32[]{:S(2)}, u32[]{:S(2)}) collective-permute-start(bf16[48,1024]{1,0:T(8,128)(2,1)S(1)} %reshape.73), channel_id=1, source_target_pairs={{0,16},{8,24},{16,0},{24,8},{1,17},{9,25},{17,1},{25,9},{2,18},{10... | collective-permute-start | bytes 294920 | tf_op jit(solution)/shard_map/ppermute | solution.py:23
  22.3 0.7 broadcast_subtract_fusion
  23.0 0.2 reshape.75
  23.2 0.1 copy.9
  23.3 0.1 reshape.76
  23.6 2.4 %collective-permute-done.2 = bf16[48,1024]{1,0:T(8,128)(2,1)S(1)} collective-permute-done((bf16[48,1024]{1,0:T(8,128)(2,1)S(1)}, bf16[48,1024]{1,0:T(8,128)(2,1)S(1)}, u32[]{:S(2)}, u32[]{:S(2)}) %collective-permute-start.2) | collective-permute-done | bytes 98336 | tf_op jit(solution)/shard_map/ppermute | solution.py:23
  26.0 3.8 %collective-permute-start.3 = (bf16[192,1024]{1,0:T(8,128)(2,1)S(1)}, bf16[192,1024]{1,0:T(8,128)(2,1)S(1)}, u32[]{:S(2)}, u32[]{:S(2)}) collective-permute-start(bf16[192,1024]{1,0:T(8,128)(2,1)S(1)} %bitcast.32), channel_id=1, source_target_pairs={{0,1},{1,0},{2,3},{3,2},{4,5},{5,4},{6,7},{7,6},{8,9},{9,8},{10,11... | collective-permute-start | bytes 1179656 | tf_op jit(solution)/shard_map/ppermute | solution.py:23
  29.8 1.3 %collective-permute-start.4 = (bf16[192,1024]{1,0:T(8,128)(2,1)S(1)}, bf16[192,1024]{1,0:T(8,128)(2,1)S(1)}, u32[]{:S(2)}, u32[]{:S(2)}) collective-permute-start(bf16[192,1024]{1,0:T(8,128)(2,1)S(1)} %bitcast.33), channel_id=1, source_target_pairs={{0,2},{2,4},{4,6},{6,0},{1,3},{3,5},{5,7},{7,1},{8,10},{10,12},{12... | collective-permute-start | bytes 1179656 | tf_op jit(solution)/shard_map/ppermute | solution.py:23
  31.1 1.4 %collective-permute-start.6 = (bf16[192,1024]{1,0:T(8,128)(2,1)S(1)}, bf16[192,1024]{1,0:T(8,128)(2,1)S(1)}, u32[]{:S(2)}, u32[]{:S(2)}) collective-permute-start(bf16[192,1024]{1,0:T(8,128)(2,1)S(1)} %bitcast.34), channel_id=1, source_target_pairs={{0,6},{2,0},{4,2},{6,4},{1,7},{3,1},{5,3},{7,5},{8,14},{10,8},{12,... | collective-permute-start | bytes 1179656 | tf_op jit(solution)/shard_map/ppermute | solution.py:23
  32.6 9.2 %collective-permute-done.4.first = bf16[192,1024]{1,0:T(8,128)(2,1)S(1)} collective-permute-done((bf16[192,1024]{1,0:T(8,128)(2,1)S(1)}, bf16[192,1024]{1,0:T(8,128)(2,1)S(1)}, u32[]{:S(2)}, u32[]{:S(2)}) %collective-permute-start.4) | collective-permute-done | bytes 393248 | tf_op jit(solution)/shard_map/ppermute | solution.py:23
  41.8 0.9 %collective-permute-start.5 = (bf16[192,1024]{1,0:T(8,128)(2,1)S(1)}, bf16[192,1024]{1,0:T(8,128)(2,1)S(1)}, u32[]{:S(2)}, u32[]{:S(2)}) collective-permute-start(bf16[192,1024]{1,0:T(8,128)(2,1)S(1)} %collective-permute-done.4.first), channel_id=1, source_target_pairs={{0,1},{1,0},{2,3},{3,2},{4,5},{5,4},{6,7},{7,6},{8,9},{9,8},{10,11... | collective-permute-start | bytes 1179656 | tf_op jit(solution)/shard_map/ppermute | solution.py:23
  42.8 1.5 %collective-permute-start.8 = (bf16[192,1024]{1,0:T(8,128)(2,1)S(1)}, bf16[192,1024]{1,0:T(8,128)(2,1)S(1)}, u32[]{:S(2)}, u32[]{:S(2)}) collective-permute-start(bf16[192,1024]{1,0:T(8,128)(2,1)S(1)} %pick.1), channel_id=1, source_target_pairs={{0,2},{1,7},{2,4},{3,1},{4,6},{5,3},{6,0},{7,5},{8,10},{9,15},{10,... | collective-permute-start | bytes 1179656 | tf_op jit(solution)/shard_map/ppermute | solution.py:33
  44.4 2.9 %score.4 = f32[2,256]{1,0:T(2,128)S(1)} custom-call(bf16[256,1024]{1,0:T(8,128)(2,1)S(1)} %pad_maximum_fusion.3.queries, bf16[4096,1024]{1,0:T(8,128)(2,1)S(1)} %bitcast.31, s32[1,256]{1,0:T(1,128)S(1)} %prep.1.targets), custom_call_target="tpu_custom_call" | custom-call | flops 2147483648 | bytes 8912896 | tf_op jit(solution)/shard_map/score/pallas_call | solution.py:82
  47.4 0.1 broadcast_select_fusion.3
  47.6 2.8 %score.6 = f32[2,256]{1,0:T(2,128)S(1)} custom-call(bf16[256,1024]{1,0:T(8,128)(2,1)S(1)} %pad_maximum_fusion.2.queries, bf16[4096,1024]{1,0:T(8,128)(2,1)S(1)} %bitcast.31, s32[1,256]{1,0:T(1,128)S(1)} %get-tuple-element.43.targets), custom_call_target="tpu_custom_call" | custom-call | flops 2147483648 | bytes 8912896 | tf_op jit(solution)/shard_map/score/pallas_call | solution.py:82
  50.4 1.4 %collective-permute-start.9 = (bf16[192,1024]{1,0:T(8,128)(2,1)S(1)}, bf16[192,1024]{1,0:T(8,128)(2,1)S(1)}, u32[]{:S(2)}, u32[]{:S(2)}) collective-permute-start(bf16[192,1024]{1,0:T(8,128)(2,1)S(1)} %collective-permute-done.8), channel_id=1, source_target_pairs={{0,1},{1,0},{2,3},{3,2},{4,5},{5,4},{6,7},{7,6},{8,9},{9,8},{10,11... | collective-permute-start | bytes 1179656 | tf_op jit(solution)/shard_map/ppermute | solution.py:23
  51.9 5.1 %score.5 = f32[2,512]{1,0:T(2,128)S(1)} custom-call(bf16[512,1024]{1,0:T(8,128)(2,1)S(1)} %pad_maximum_fusion.queries, bf16[4096,1024]{1,0:T(8,128)(2,1)S(1)} %bitcast.31, s32[1,512]{1,0:T(1,128)S(1)} %get-tuple-element.42.targets), custom_call_target="tpu_custom_call" | custom-call | flops 4294967296 | bytes 9437184 | tf_op jit(solution)/shard_map/score/pallas_call | solution.py:82
  57.0 0.1 pad_maximum_fusion.1.queries
  57.1 5.1 %score.7 = f32[2,512]{1,0:T(2,128)S(1)} custom-call(bf16[512,1024]{1,0:T(8,128)(2,1)S(1)} %pad_maximum_fusion.1.queries, bf16[4096,1024]{1,0:T(8,128)(2,1)S(1)} %bitcast.31, s32[1,512]{1,0:T(1,128)S(1)} %get-tuple-element.45.targets), custom_call_target="tpu_custom_call" | custom-call | flops 4294967296 | bytes 9437184 | tf_op jit(solution)/shard_map/score/pallas_call | solution.py:82
  62.4 0.1 collective-permute-start.10
  62.5 1.1 %collective-permute-done.10 = f32[2,1536]{1,0:T(2,128)S(1)} collective-permute-done((f32[2,1536]{1,0:T(2,128)S(1)}, f32[2,1536]{1,0:T(2,128)S(1)}, u32[]{:S(2)}, u32[]{:S(2)}) %collective-permute-start.10) | collective-permute-done | bytes 12320 | tf_op jit(solution)/shard_map/ppermute | solution.py:23
  63.9 11.0 %all_to_all.16 = f32[16,2,1536]{2,1,0:T(2,128)S(1)} all-to-all(f32[16,2,1536]{2,1,0:T(2,128)S(1)} %broadcast_in_dim.42), channel_id=1, replica_groups=mesh['group'=8,'x'=4,'y'=4,'core'=2] {'x','y'}, dimensions={0} | all-to-all | bytes 393216 | tf_op jit(solution)/shard_map/all_to_all | solution.py:18
  74.9 0.2 slice_reduce_fusion.1
  75.2 10.0 %all_to_all.17.parts = f32[8,2,1536]{2,1,0:T(2,128)S(1)} all-to-all(f32[8,2,1536]{2,1,0:T(2,128)S(1)} %broadcast_in_dim.43), channel_id=1, replica_groups=mesh['group'=8,'x'=4,'y'=4,'core'=2] {'group'}, dimensions={0} | all-to-all | bytes 196608 | tf_op jit(solution)/shard_map/all_to_all | solution.py:18
  85.2 0.7 close.1
  85.9 0.1 reshape.79
  86.1 0.1 copy.12
  86.2 0.8 reshape.80
  (57 shorter events, 1.1 us)
Async XLA Ops:
  18.0 5.6 %collective-permute-start = (bf16[48,1024]{1,0:T(8,128)(2,1)S(1)}, bf16[48,1024]{1,0:T(8,128)(2,1)S(1)}, u32[]{:S(2)}, u32[]{:S(2)}) collective-permute-start(bf16[48,1024]{1,0:T(8,128)(2,1)S(1)} %reshape.73), channel_id=1, source_target_pairs={{0,8},{8,16},{16,24},{24,0},{1,9},{9,17},{17,25},{25,1},{2,10},{10... | collective-permute-start | bytes 294920 | tf_op jit(solution)/shard_map/ppermute | solution.py:23
  19.3 4.3 %collective-permute-start.1 = (bf16[48,1024]{1,0:T(8,128)(2,1)S(1)}, bf16[48,1024]{1,0:T(8,128)(2,1)S(1)}, u32[]{:S(2)}, u32[]{:S(2)}) collective-permute-start(bf16[48,1024]{1,0:T(8,128)(2,1)S(1)} %reshape.73), channel_id=1, source_target_pairs={{0,24},{8,0},{16,8},{24,16},{1,25},{9,1},{17,9},{25,17},{2,26},{10... | collective-permute-start | bytes 294920 | tf_op jit(solution)/shard_map/ppermute | solution.py:23
  20.7 5.3 %collective-permute-start.2 = (bf16[48,1024]{1,0:T(8,128)(2,1)S(1)}, bf16[48,1024]{1,0:T(8,128)(2,1)S(1)}, u32[]{:S(2)}, u32[]{:S(2)}) collective-permute-start(bf16[48,1024]{1,0:T(8,128)(2,1)S(1)} %reshape.73), channel_id=1, source_target_pairs={{0,16},{8,24},{16,0},{24,8},{1,17},{9,25},{17,1},{25,9},{2,18},{10... | collective-permute-start | bytes 294920 | tf_op jit(solution)/shard_map/ppermute | solution.py:23
  26.0 18.4 %slice-start = ((s8[8388608]{0:T(1024)(128)(4,1)}), s8[4194304]{0:T(1024)(128)(4,1)S(1)}, s32[]{:S(2)}) async-start(s8[8388608]{0:T(1024)(128)(4,1)} %bitcast.30), calls=%async_computation.3 | async-start | bytes 8388608
  26.0 18.4 %slice-start.1 = ((s8[8388608]{0:T(1024)(128)(4,1)}), s8[4194304]{0:T(1024)(128)(4,1)S(1)}, s32[]{:S(2)}) async-start(s8[8388608]{0:T(1024)(128)(4,1)} %bitcast.30), calls=%async_computation.4 | async-start | bytes 8388608
  26.0 16.6 %collective-permute-start.3 = (bf16[192,1024]{1,0:T(8,128)(2,1)S(1)}, bf16[192,1024]{1,0:T(8,128)(2,1)S(1)}, u32[]{:S(2)}, u32[]{:S(2)}) collective-permute-start(bf16[192,1024]{1,0:T(8,128)(2,1)S(1)} %bitcast.32), channel_id=1, source_target_pairs={{0,1},{1,0},{2,3},{3,2},{4,5},{5,4},{6,7},{7,6},{8,9},{9,8},{10,11... | collective-permute-start | bytes 1179656 | tf_op jit(solution)/shard_map/ppermute | solution.py:23
  29.8 11.9 %collective-permute-start.4 = (bf16[192,1024]{1,0:T(8,128)(2,1)S(1)}, bf16[192,1024]{1,0:T(8,128)(2,1)S(1)}, u32[]{:S(2)}, u32[]{:S(2)}) collective-permute-start(bf16[192,1024]{1,0:T(8,128)(2,1)S(1)} %bitcast.33), channel_id=1, source_target_pairs={{0,2},{2,4},{4,6},{6,0},{1,3},{3,5},{5,7},{7,1},{8,10},{10,12},{12... | collective-permute-start | bytes 1179656 | tf_op jit(solution)/shard_map/ppermute | solution.py:23
  31.1 11.6 %collective-permute-start.6 = (bf16[192,1024]{1,0:T(8,128)(2,1)S(1)}, bf16[192,1024]{1,0:T(8,128)(2,1)S(1)}, u32[]{:S(2)}, u32[]{:S(2)}) collective-permute-start(bf16[192,1024]{1,0:T(8,128)(2,1)S(1)} %bitcast.34), channel_id=1, source_target_pairs={{0,6},{2,0},{4,2},{6,4},{1,7},{3,1},{5,3},{7,5},{8,14},{10,8},{12,... | collective-permute-start | bytes 1179656 | tf_op jit(solution)/shard_map/ppermute | solution.py:23
  41.8 5.5 %collective-permute-start.5 = (bf16[192,1024]{1,0:T(8,128)(2,1)S(1)}, bf16[192,1024]{1,0:T(8,128)(2,1)S(1)}, u32[]{:S(2)}, u32[]{:S(2)}) collective-permute-start(bf16[192,1024]{1,0:T(8,128)(2,1)S(1)} %collective-permute-done.4.first), channel_id=1, source_target_pairs={{0,1},{1,0},{2,3},{3,2},{4,5},{5,4},{6,7},{7,6},{8,9},{9,8},{10,11... | collective-permute-start | bytes 1179656 | tf_op jit(solution)/shard_map/ppermute | solution.py:23
  42.8 7.6 %collective-permute-start.8 = (bf16[192,1024]{1,0:T(8,128)(2,1)S(1)}, bf16[192,1024]{1,0:T(8,128)(2,1)S(1)}, u32[]{:S(2)}, u32[]{:S(2)}) collective-permute-start(bf16[192,1024]{1,0:T(8,128)(2,1)S(1)} %pick.1), channel_id=1, source_target_pairs={{0,2},{1,7},{2,4},{3,1},{4,6},{5,3},{6,0},{7,5},{8,10},{9,15},{10,... | collective-permute-start | bytes 1179656 | tf_op jit(solution)/shard_map/ppermute | solution.py:33
  44.3 3.0 %collective-permute-start.7 = (bf16[192,1024]{1,0:T(8,128)(2,1)S(1)}, bf16[192,1024]{1,0:T(8,128)(2,1)S(1)}, u32[]{:S(2)}, u32[]{:S(2)}) collective-permute-start(bf16[192,1024]{1,0:T(8,128)(2,1)S(1)} %collective-permute-done.6.second), channel_id=1, source_target_pairs={{0,1},{1,0},{2,3},{3,2},{4,5},{5,4},{6,7},{7,6},{8,9},{9,8},{10,11... | collective-permute-start | bytes 1179656 | tf_op jit(solution)/shard_map/ppermute | solution.py:23
  50.4 6.5 %collective-permute-start.9 = (bf16[192,1024]{1,0:T(8,128)(2,1)S(1)}, bf16[192,1024]{1,0:T(8,128)(2,1)S(1)}, u32[]{:S(2)}, u32[]{:S(2)}) collective-permute-start(bf16[192,1024]{1,0:T(8,128)(2,1)S(1)} %collective-permute-done.8), channel_id=1, source_target_pairs={{0,1},{1,0},{2,3},{3,2},{4,5},{5,4},{6,7},{7,6},{8,9},{9,8},{10,11... | collective-permute-start | bytes 1179656 | tf_op jit(solution)/shard_map/ppermute | solution.py:23
  62.4 1.3 %collective-permute-start.10 = (f32[2,1536]{1,0:T(2,128)S(1)}, f32[2,1536]{1,0:T(2,128)S(1)}, u32[]{:S(2)}, u32[]{:S(2)}) collective-permute-start(f32[2,1536]{1,0:T(2,128)S(1)} %bitcast.39), channel_id=1, source_target_pairs={{0,1},{1,0},{2,3},{3,2},{4,5},{5,4},{6,7},{7,6},{8,9},{9,8},{10,11... | collective-permute-start | bytes 36872 | tf_op jit(solution)/shard_map/ppermute | solution.py:23

commit v6 on v5

--- a/solution.py
+++ b/solution.py
@@ -144,6 +144,30 @@
     top = jnp.max(lse, axis=0)
     lse = top + jnp.log(jnp.sum(jnp.exp(lse - top), axis=0))
     return jnp.stack([lse, jnp.sum(picked, axis=0)])
+
+
+def join_kernel(parts, out):
+    lse, picked = parts[:, 0, :], parts[:, 1, :]
+    top = jnp.max(lse, axis=0, keepdims=True)
+    total = jnp.sum(jnp.exp(lse - top), axis=0, keepdims=True)
+    lse, picked = top + jnp.log(total), jnp.sum(picked, axis=0, keepdims=True)
+    for peer in range(out.shape[0]):
+        out[peer, 0:1, :] = lse
+        out[peer, 1:2, :] = picked
+
+
+def joined(parts, axis):
+    size = lax.axis_size(axis)
+    vmem = pl.BlockSpec(memory_space=pltpu.VMEM)
+    copies = pl.pallas_call(
+        join_kernel,
+        out_shape=jax.ShapeDtypeStruct((size, *parts.shape[1:]), parts.dtype),
+        in_specs=[vmem],
+        out_specs=vmem,
+        compiler_params=pltpu.CompilerParams(vmem_limit_bytes=4 * 2**20),
+        name="join",
+    )(parts)
+    return lax.all_to_all(copies, axis, split_axis=0, concat_axis=0, tiled=True)
 
 
 def close_kernel(parts, losses, mean):
@@ -226,8 +250,8 @@
         found = lax.dynamic_update_index_in_dim(found, parts[:, place], y_place[step], 1)
     partial = found.reshape(2, -1)
     partial = merge(jnp.stack([partial, shifted(partial, "core", 1)]))
-    partial = merge(broadcast_to_peers(partial, ("x", "y")))
-    losses, mean = closed(broadcast_to_peers(partial, "group"))
+    partial = broadcast_to_peers(partial, ("x", "y"))
+    losses, mean = closed(joined(partial, "group"))
     losses = losses.reshape(ys, cores, xs, groups, each).transpose(3, 2, 0, 1, 4).reshape(-1)
     return (losses, mean.reshape(()))
 

time: 87.7 us -> 87.4 us (level)
    all_to_all x0 -> x1, blocking collectives: none -> 10 us  [joined(): return lax.all_to_all(copies, axis, split_axis=0, concat_axis=0, tiled=True)]
    all_to_all x3 -> x2, blocking collectives: 37.6 us -> 27.5 us  [broadcast_to_peers(): return lax.all_to_all(copies, axis, split_axis=0, concat_axis=0, tiled=True)]
where the time goes in v6:
time: 87.4 us; the launch traced here: 86.7 us
  blocking collectives  37.6 us (43%)
  Pallas kernels  16.6 us (19%)
  starting transfers between devices  14.8 us (17%)
  waiting for transfers between devices  12.7 us (15%)
  local copies, waits for them, and re-layouts  2.69 us (3%)
  other arithmetic  1.32 us (2%)
  between operations  1.02 us (1%)
    all_to_all x2, blocking collectives, broadcast_to_peers(): return lax.all_to_all(copies, axis, split_axis=0, concat_axis=0, tiled=True)  27.5 us
    pallas_call x4, Pallas kernels, score(): pl.pallas_call(functools.partial(score_kernel, tiles), out_shape=jax.Shap...  15.8 us
    ppermute x10, starting transfers between devices, shifted(): lax.ppermute(value, axis, [(k, (k + step) % size) for k in range(size)])  13.3 us
    ppermute x10, waiting for transfers between devices, shifted(): lax.ppermute(value, axis, [(k, (k + step) % size) for k in range(size)])  12.7 us
    all_to_all x1, blocking collectives, joined(): return lax.all_to_all(copies, axis, split_axis=0, concat_axis=0, tiled=True)  10 us
  transfers between devices with their start and end apart: 11, of which 3 were waited for; matrix products, arithmetic and copies ran while one was open for 2% of the time, Pallas kernels for 12%

profile of v6, /device:TPU:1, one launch (start us, length us, event | category | flops | bytes accessed | tf_op | source)
XLA Modules:
  0.0 86.7 jit_solution(11175469833116141022)
XLA Ops:
  0.7 0.7 broadcast_in_dim.33
  1.4 16.6 %all_to_all.15 = bf16[8,6,1024]{2,1,0:T(8,128)(2,1)S(1)} all-to-all(bf16[8,6,1024]{2,1,0:T(8,128)(2,1)S(1)} %broadcast_in_dim.33), channel_id=1, replica_groups=mesh['group'=8,'x'=4,'y'=4,'core'=2] {'group'}, dimensions={0} | all-to-all | bytes 196608 | tf_op jit(solution)/shard_map/all_to_all | solution.py:18
  18.0 1.3 %collective-permute-start = (bf16[48,1024]{1,0:T(8,128)(2,1)S(1)}, bf16[48,1024]{1,0:T(8,128)(2,1)S(1)}, u32[]{:S(2)}, u32[]{:S(2)}) collective-permute-start(bf16[48,1024]{1,0:T(8,128)(2,1)S(1)} %reshape.56), channel_id=1, source_target_pairs={{0,8},{8,16},{16,24},{24,0},{1,9},{9,17},{17,25},{25,1},{2,10},{10... | collective-permute-start | bytes 294920 | tf_op jit(solution)/shard_map/ppermute | solution.py:23
  19.3 1.5 %collective-permute-start.1 = (bf16[48,1024]{1,0:T(8,128)(2,1)S(1)}, bf16[48,1024]{1,0:T(8,128)(2,1)S(1)}, u32[]{:S(2)}, u32[]{:S(2)}) collective-permute-start(bf16[48,1024]{1,0:T(8,128)(2,1)S(1)} %reshape.56), channel_id=1, source_target_pairs={{0,24},{8,0},{16,8},{24,16},{1,25},{9,1},{17,9},{25,17},{2,26},{10... | collective-permute-start | bytes 294920 | tf_op jit(solution)/shard_map/ppermute | solution.py:23
  20.7 1.5 %collective-permute-start.2 = (bf16[48,1024]{1,0:T(8,128)(2,1)S(1)}, bf16[48,1024]{1,0:T(8,128)(2,1)S(1)}, u32[]{:S(2)}, u32[]{:S(2)}) collective-permute-start(bf16[48,1024]{1,0:T(8,128)(2,1)S(1)} %reshape.56), channel_id=1, source_target_pairs={{0,16},{8,24},{16,0},{24,8},{1,17},{9,25},{17,1},{25,9},{2,18},{10... | collective-permute-start | bytes 294920 | tf_op jit(solution)/shard_map/ppermute | solution.py:23
  22.3 0.7 broadcast_subtract_fusion
  23.0 0.2 reshape.58
  23.2 0.1 copy.5
  23.3 0.1 reshape.59
  23.6 2.4 %collective-permute-done.2 = bf16[48,1024]{1,0:T(8,128)(2,1)S(1)} collective-permute-done((bf16[48,1024]{1,0:T(8,128)(2,1)S(1)}, bf16[48,1024]{1,0:T(8,128)(2,1)S(1)}, u32[]{:S(2)}, u32[]{:S(2)}) %collective-permute-start.2) | collective-permute-done | bytes 98336 | tf_op jit(solution)/shard_map/ppermute | solution.py:23
  26.0 3.8 %collective-permute-start.3 = (bf16[192,1024]{1,0:T(8,128)(2,1)S(1)}, bf16[192,1024]{1,0:T(8,128)(2,1)S(1)}, u32[]{:S(2)}, u32[]{:S(2)}) collective-permute-start(bf16[192,1024]{1,0:T(8,128)(2,1)S(1)} %bitcast.26), channel_id=1, source_target_pairs={{0,1},{1,0},{2,3},{3,2},{4,5},{5,4},{6,7},{7,6},{8,9},{9,8},{10,11... | collective-permute-start | bytes 1179656 | tf_op jit(solution)/shard_map/ppermute | solution.py:23
  29.8 1.3 %collective-permute-start.4 = (bf16[192,1024]{1,0:T(8,128)(2,1)S(1)}, bf16[192,1024]{1,0:T(8,128)(2,1)S(1)}, u32[]{:S(2)}, u32[]{:S(2)}) collective-permute-start(bf16[192,1024]{1,0:T(8,128)(2,1)S(1)} %bitcast.27), channel_id=1, source_target_pairs={{0,2},{2,4},{4,6},{6,0},{1,3},{3,5},{5,7},{7,1},{8,10},{10,12},{12... | collective-permute-start | bytes 1179656 | tf_op jit(solution)/shard_map/ppermute | solution.py:23
  31.1 1.4 %collective-permute-start.6 = (bf16[192,1024]{1,0:T(8,128)(2,1)S(1)}, bf16[192,1024]{1,0:T(8,128)(2,1)S(1)}, u32[]{:S(2)}, u32[]{:S(2)}) collective-permute-start(bf16[192,1024]{1,0:T(8,128)(2,1)S(1)} %bitcast.28), channel_id=1, source_target_pairs={{0,6},{2,0},{4,2},{6,4},{1,7},{3,1},{5,3},{7,5},{8,14},{10,8},{12,... | collective-permute-start | bytes 1179656 | tf_op jit(solution)/shard_map/ppermute | solution.py:23
  32.6 9.2 %collective-permute-done.4.first = bf16[192,1024]{1,0:T(8,128)(2,1)S(1)} collective-permute-done((bf16[192,1024]{1,0:T(8,128)(2,1)S(1)}, bf16[192,1024]{1,0:T(8,128)(2,1)S(1)}, u32[]{:S(2)}, u32[]{:S(2)}) %collective-permute-start.4) | collective-permute-done | bytes 393248 | tf_op jit(solution)/shard_map/ppermute | solution.py:23
  41.8 0.9 %collective-permute-start.5 = (bf16[192,1024]{1,0:T(8,128)(2,1)S(1)}, bf16[192,1024]{1,0:T(8,128)(2,1)S(1)}, u32[]{:S(2)}, u32[]{:S(2)}) collective-permute-start(bf16[192,1024]{1,0:T(8,128)(2,1)S(1)} %collective-permute-done.4.first), channel_id=1, source_target_pairs={{0,1},{1,0},{2,3},{3,2},{4,5},{5,4},{6,7},{7,6},{8,9},{9,8},{10,11... | collective-permute-start | bytes 1179656 | tf_op jit(solution)/shard_map/ppermute | solution.py:23
  42.8 1.5 %collective-permute-start.8 = (bf16[192,1024]{1,0:T(8,128)(2,1)S(1)}, bf16[192,1024]{1,0:T(8,128)(2,1)S(1)}, u32[]{:S(2)}, u32[]{:S(2)}) collective-permute-start(bf16[192,1024]{1,0:T(8,128)(2,1)S(1)} %pick.1), channel_id=1, source_target_pairs={{0,2},{1,7},{2,4},{3,1},{4,6},{5,3},{6,0},{7,5},{8,10},{9,15},{10,... | collective-permute-start | bytes 1179656 | tf_op jit(solution)/shard_map/ppermute | solution.py:33
  44.4 2.9 %score.4 = f32[2,256]{1,0:T(2,128)S(1)} custom-call(bf16[256,1024]{1,0:T(8,128)(2,1)S(1)} %pad_maximum_fusion.3.queries, bf16[4096,1024]{1,0:T(8,128)(2,1)S(1)} %bitcast.25, s32[1,256]{1,0:T(1,128)S(1)} %prep.1.targets), custom_call_target="tpu_custom_call" | custom-call | flops 2147483648 | bytes 8912896 | tf_op jit(solution)/shard_map/score/pallas_call | solution.py:82
  47.4 0.1 broadcast_select_fusion.3
  47.6 2.8 %score.6 = f32[2,256]{1,0:T(2,128)S(1)} custom-call(bf16[256,1024]{1,0:T(8,128)(2,1)S(1)} %pad_maximum_fusion.2.queries, bf16[4096,1024]{1,0:T(8,128)(2,1)S(1)} %bitcast.25, s32[1,256]{1,0:T(1,128)S(1)} %get-tuple-element.43.targets), custom_call_target="tpu_custom_call" | custom-call | flops 2147483648 | bytes 8912896 | tf_op jit(solution)/shard_map/score/pallas_call | solution.py:82
  50.4 1.4 %collective-permute-start.9 = (bf16[192,1024]{1,0:T(8,128)(2,1)S(1)}, bf16[192,1024]{1,0:T(8,128)(2,1)S(1)}, u32[]{:S(2)}, u32[]{:S(2)}) collective-permute-start(bf16[192,1024]{1,0:T(8,128)(2,1)S(1)} %collective-permute-done.8), channel_id=1, source_target_pairs={{0,1},{1,0},{2,3},{3,2},{4,5},{5,4},{6,7},{7,6},{8,9},{9,8},{10,11... | collective-permute-start | bytes 1179656 | tf_op jit(solution)/shard_map/ppermute | solution.py:23
  51.9 5.1 %score.5 = f32[2,512]{1,0:T(2,128)S(1)} custom-call(bf16[512,1024]{1,0:T(8,128)(2,1)S(1)} %pad_maximum_fusion.queries, bf16[4096,1024]{1,0:T(8,128)(2,1)S(1)} %bitcast.25, s32[1,512]{1,0:T(1,128)S(1)} %get-tuple-element.42.targets), custom_call_target="tpu_custom_call" | custom-call | flops 4294967296 | bytes 9437184 | tf_op jit(solution)/shard_map/score/pallas_call | solution.py:82
  57.0 0.1 pad_maximum_fusion.1.queries
  57.1 5.1 %score.7 = f32[2,512]{1,0:T(2,128)S(1)} custom-call(bf16[512,1024]{1,0:T(8,128)(2,1)S(1)} %pad_maximum_fusion.1.queries, bf16[4096,1024]{1,0:T(8,128)(2,1)S(1)} %bitcast.25, s32[1,512]{1,0:T(1,128)S(1)} %get-tuple-element.45.targets), custom_call_target="tpu_custom_call" | custom-call | flops 4294967296 | bytes 9437184 | tf_op jit(solution)/shard_map/score/pallas_call | solution.py:82
  62.4 0.1 collective-permute-start.10
  62.5 1.1 %collective-permute-done.10 = f32[2,1536]{1,0:T(2,128)S(1)} collective-permute-done((f32[2,1536]{1,0:T(2,128)S(1)}, f32[2,1536]{1,0:T(2,128)S(1)}, u32[]{:S(2)}, u32[]{:S(2)}) %collective-permute-start.10) | collective-permute-done | bytes 12320 | tf_op jit(solution)/shard_map/ppermute | solution.py:23
  63.9 11.0 %all_to_all.16.parts = f32[16,2,1536]{2,1,0:T(2,128)S(1)} all-to-all(f32[16,2,1536]{2,1,0:T(2,128)S(1)} %broadcast_in_dim.38), channel_id=1, replica_groups=mesh['group'=8,'x'=4,'y'=4,'core'=2] {'x','y'}, dimensions={0} | all-to-all | bytes 393216 | tf_op jit(solution)/shard_map/all_to_all | solution.py:18
  74.9 0.1 join.1
  75.0 10.0 %all_to_all.17.parts = f32[8,2,1536]{2,1,0:T(2,128)S(1)} all-to-all(f32[8,2,1536]{2,1,0:T(2,128)S(1)} %join.1), channel_id=1, replica_groups=mesh['group'=8,'x'=4,'y'=4,'core'=2] {'group'}, dimensions={0} | all-to-all | bytes 196608 | tf_op jit(solution)/shard_map/all_to_all | solution.py:170
  85.0 0.7 close.1
  85.7 0.1 reshape.62
  85.8 0.1 copy.6
  85.9 0.8 reshape.63
  (51 shorter events, 1.0 us)
Async XLA Ops:
  18.0 5.6 %collective-permute-start = (bf16[48,1024]{1,0:T(8,128)(2,1)S(1)}, bf16[48,1024]{1,0:T(8,128)(2,1)S(1)}, u32[]{:S(2)}, u32[]{:S(2)}) collective-permute-start(bf16[48,1024]{1,0:T(8,128)(2,1)S(1)} %reshape.56), channel_id=1, source_target_pairs={{0,8},{8,16},{16,24},{24,0},{1,9},{9,17},{17,25},{25,1},{2,10},{10... | collective-permute-start | bytes 294920 | tf_op jit(solution)/shard_map/ppermute | solution.py:23
  19.3 4.3 %collective-permute-start.1 = (bf16[48,1024]{1,0:T(8,128)(2,1)S(1)}, bf16[48,1024]{1,0:T(8,128)(2,1)S(1)}, u32[]{:S(2)}, u32[]{:S(2)}) collective-permute-start(bf16[48,1024]{1,0:T(8,128)(2,1)S(1)} %reshape.56), channel_id=1, source_target_pairs={{0,24},{8,0},{16,8},{24,16},{1,25},{9,1},{17,9},{25,17},{2,26},{10... | collective-permute-start | bytes 294920 | tf_op jit(solution)/shard_map/ppermute | solution.py:23
  20.7 5.3 %collective-permute-start.2 = (bf16[48,1024]{1,0:T(8,128)(2,1)S(1)}, bf16[48,1024]{1,0:T(8,128)(2,1)S(1)}, u32[]{:S(2)}, u32[]{:S(2)}) collective-permute-start(bf16[48,1024]{1,0:T(8,128)(2,1)S(1)} %reshape.56), channel_id=1, source_target_pairs={{0,16},{8,24},{16,0},{24,8},{1,17},{9,25},{17,1},{25,9},{2,18},{10... | collective-permute-start | bytes 294920 | tf_op jit(solution)/shard_map/ppermute | solution.py:23
  26.0 18.4 %slice-start = ((s8[8388608]{0:T(1024)(128)(4,1)}), s8[4194304]{0:T(1024)(128)(4,1)S(1)}, s32[]{:S(2)}) async-start(s8[8388608]{0:T(1024)(128)(4,1)} %bitcast.24), calls=%async_computation.3 | async-start | bytes 8388608
  26.0 18.4 %slice-start.1 = ((s8[8388608]{0:T(1024)(128)(4,1)}), s8[4194304]{0:T(1024)(128)(4,1)S(1)}, s32[]{:S(2)}) async-start(s8[8388608]{0:T(1024)(128)(4,1)} %bitcast.24), calls=%async_computation.4 | async-start | bytes 8388608
  26.0 16.6 %collective-permute-start.3 = (bf16[192,1024]{1,0:T(8,128)(2,1)S(1)}, bf16[192,1024]{1,0:T(8,128)(2,1)S(1)}, u32[]{:S(2)}, u32[]{:S(2)}) collective-permute-start(bf16[192,1024]{1,0:T(8,128)(2,1)S(1)} %bitcast.26), channel_id=1, source_target_pairs={{0,1},{1,0},{2,3},{3,2},{4,5},{5,4},{6,7},{7,6},{8,9},{9,8},{10,11... | collective-permute-start | bytes 1179656 | tf_op jit(solution)/shard_map/ppermute | solution.py:23
  29.8 11.9 %collective-permute-start.4 = (bf16[192,1024]{1,0:T(8,128)(2,1)S(1)}, bf16[192,1024]{1,0:T(8,128)(2,1)S(1)}, u32[]{:S(2)}, u32[]{:S(2)}) collective-permute-start(bf16[192,1024]{1,0:T(8,128)(2,1)S(1)} %bitcast.27), channel_id=1, source_target_pairs={{0,2},{2,4},{4,6},{6,0},{1,3},{3,5},{5,7},{7,1},{8,10},{10,12},{12... | collective-permute-start | bytes 1179656 | tf_op jit(solution)/shard_map/ppermute | solution.py:23
  31.1 11.6 %collective-permute-start.6 = (bf16[192,1024]{1,0:T(8,128)(2,1)S(1)}, bf16[192,1024]{1,0:T(8,128)(2,1)S(1)}, u32[]{:S(2)}, u32[]{:S(2)}) collective-permute-start(bf16[192,1024]{1,0:T(8,128)(2,1)S(1)} %bitcast.28), channel_id=1, source_target_pairs={{0,6},{2,0},{4,2},{6,4},{1,7},{3,1},{5,3},{7,5},{8,14},{10,8},{12,... | collective-permute-start | bytes 1179656 | tf_op jit(solution)/shard_map/ppermute | solution.py:23
  41.8 5.5 %collective-permute-start.5 = (bf16[192,1024]{1,0:T(8,128)(2,1)S(1)}, bf16[192,1024]{1,0:T(8,128)(2,1)S(1)}, u32[]{:S(2)}, u32[]{:S(2)}) collective-permute-start(bf16[192,1024]{1,0:T(8,128)(2,1)S(1)} %collective-permute-done.4.first), channel_id=1, source_target_pairs={{0,1},{1,0},{2,3},{3,2},{4,5},{5,4},{6,7},{7,6},{8,9},{9,8},{10,11... | collective-permute-start | bytes 1179656 | tf_op jit(solution)/shard_map/ppermute | solution.py:23
  42.8 7.6 %collective-permute-start.8 = (bf16[192,1024]{1,0:T(8,128)(2,1)S(1)}, bf16[192,1024]{1,0:T(8,128)(2,1)S(1)}, u32[]{:S(2)}, u32[]{:S(2)}) collective-permute-start(bf16[192,1024]{1,0:T(8,128)(2,1)S(1)} %pick.1), channel_id=1, source_target_pairs={{0,2},{1,7},{2,4},{3,1},{4,6},{5,3},{6,0},{7,5},{8,10},{9,15},{10,... | collective-permute-start | bytes 1179656 | tf_op jit(solution)/shard_map/ppermute | solution.py:33
  44.3 3.0 %collective-permute-start.7 = (bf16[192,1024]{1,0:T(8,128)(2,1)S(1)}, bf16[192,1024]{1,0:T(8,128)(2,1)S(1)}, u32[]{:S(2)}, u32[]{:S(2)}) collective-permute-start(bf16[192,1024]{1,0:T(8,128)(2,1)S(1)} %collective-permute-done.6.second), channel_id=1, source_target_pairs={{0,1},{1,0},{2,3},{3,2},{4,5},{5,4},{6,7},{7,6},{8,9},{9,8},{10,11... | collective-permute-start | bytes 1179656 | tf_op jit(solution)/shard_map/ppermute | solution.py:23
  50.4 6.5 %collective-permute-start.9 = (bf16[192,1024]{1,0:T(8,128)(2,1)S(1)}, bf16[192,1024]{1,0:T(8,128)(2,1)S(1)}, u32[]{:S(2)}, u32[]{:S(2)}) collective-permute-start(bf16[192,1024]{1,0:T(8,128)(2,1)S(1)} %collective-permute-done.8), channel_id=1, source_target_pairs={{0,1},{1,0},{2,3},{3,2},{4,5},{5,4},{6,7},{7,6},{8,9},{9,8},{10,11... | collective-permute-start | bytes 1179656 | tf_op jit(solution)/shard_map/ppermute | solution.py:23
  62.4 1.3 %collective-permute-start.10 = (f32[2,1536]{1,0:T(2,128)S(1)}, f32[2,1536]{1,0:T(2,128)S(1)}, u32[]{:S(2)}, u32[]{:S(2)}) collective-permute-start(f32[2,1536]{1,0:T(2,128)S(1)} %bitcast.33), channel_id=1, source_target_pairs={{0,1},{1,0},{2,3},{3,2},{4,5},{5,4},{6,7},{7,6},{8,9},{9,8},{10,11... | collective-permute-start | bytes 36872 | tf_op jit(solution)/shard_map/ppermute | solution.py:23

commit v7 on v6

--- a/solution.py
+++ b/solution.py
@@ -137,13 +137,6 @@
         cost_estimate=pl.CostEstimate(flops=2 * 10**10, bytes_accessed=4096, transcendentals=0),
         name="prep",
     )(value)
-
-
-def merge(parts):
-    lse, picked = parts[:, 0], parts[:, 1]
-    top = jnp.max(lse, axis=0)
-    lse = top + jnp.log(jnp.sum(jnp.exp(lse - top), axis=0))
-    return jnp.stack([lse, jnp.sum(picked, axis=0)])
 
 
 def join_kernel(parts, out):
@@ -249,8 +242,7 @@
     for place, step in enumerate((0, 1, ys - 1, 2)):
         found = lax.dynamic_update_index_in_dim(found, parts[:, place], y_place[step], 1)
     partial = found.reshape(2, -1)
-    partial = merge(jnp.stack([partial, shifted(partial, "core", 1)]))
-    partial = broadcast_to_peers(partial, ("x", "y"))
+    partial = joined(jnp.stack([partial, shifted(partial, "core", 1)]), ("x", "y"))
     losses, mean = closed(joined(partial, "group"))
     losses = losses.reshape(ys, cores, xs, groups, each).transpose(3, 2, 0, 1, 4).reshape(-1)
     return (losses, mean.reshape(()))

time: 87.4 us -> 87.3 us (level)
    all_to_all x2 -> x1, blocking collectives: 27.5 us -> 16.6 us  [broadcast_to_peers(): return lax.all_to_all(copies, axis, split_axis=0, concat_axis=0, tiled=True)]
    all_to_all x1 -> x2, blocking collectives: 10 us -> 21 us  [joined(): return lax.all_to_all(copies, axis, split_axis=0, concat_axis=0, tiled=True)]
where the time goes in v7:
time: 87.3 us; the launch traced here: 86.6 us
  blocking collectives  37.6 us (43%)
  Pallas kernels  16.6 us (19%)
  starting transfers between devices  14.8 us (17%)
  waiting for transfers between devices  12.7 us (15%)
  local copies, waits for them, and re-layouts  2.62 us (3%)
  other arithmetic  1.23 us (1%)
  between operations  0.98 us (1%)
    all_to_all x2, blocking collectives, joined(): return lax.all_to_all(copies, axis, split_axis=0, concat_axis=0, tiled=True)  21 us
    all_to_all x1, blocking collectives, broadcast_to_peers(): return lax.all_to_all(copies, axis, split_axis=0, concat_axis=0, tiled=True)  16.6 us
    pallas_call x4, Pallas kernels, score(): pl.pallas_call(functools.partial(score_kernel, tiles), out_shape=jax.Shap...  15.8 us
    ppermute x10, starting transfers between devices, shifted(): lax.ppermute(value, axis, [(k, (k + step) % size) for k in range(size)])  13.3 us
    ppermute x10, waiting for transfers between devices, shifted(): lax.ppermute(value, axis, [(k, (k + step) % size) for k in range(size)])  12.7 us
  transfers between devices with their start and end apart: 11, of which 3 were waited for; matrix products, arithmetic and copies ran while one was open for 2% of the time, Pallas kernels for 12%

profile of v7, /device:TPU:1, one launch (start us, length us, event | category | flops | bytes accessed | tf_op | source)
XLA Modules:
  0.0 86.6 jit_solution(4995374182717747981)
XLA Ops:
  0.7 0.7 broadcast_in_dim.29
  1.4 16.6 %all_to_all.15 = bf16[8,6,1024]{2,1,0:T(8,128)(2,1)S(1)} all-to-all(bf16[8,6,1024]{2,1,0:T(8,128)(2,1)S(1)} %broadcast_in_dim.29), channel_id=1, replica_groups=mesh['group'=8,'x'=4,'y'=4,'core'=2] {'group'}, dimensions={0} | all-to-all | bytes 196608 | tf_op jit(solution)/shard_map/all_to_all | solution.py:18
  18.0 1.3 %collective-permute-start = (bf16[48,1024]{1,0:T(8,128)(2,1)S(1)}, bf16[48,1024]{1,0:T(8,128)(2,1)S(1)}, u32[]{:S(2)}, u32[]{:S(2)}) collective-permute-start(bf16[48,1024]{1,0:T(8,128)(2,1)S(1)} %reshape.39), channel_id=1, source_target_pairs={{0,8},{8,16},{16,24},{24,0},{1,9},{9,17},{17,25},{25,1},{2,10},{10... | collective-permute-start | bytes 294920 | tf_op jit(solution)/shard_map/ppermute | solution.py:23
  19.3 1.5 %collective-permute-start.1 = (bf16[48,1024]{1,0:T(8,128)(2,1)S(1)}, bf16[48,1024]{1,0:T(8,128)(2,1)S(1)}, u32[]{:S(2)}, u32[]{:S(2)}) collective-permute-start(bf16[48,1024]{1,0:T(8,128)(2,1)S(1)} %reshape.39), channel_id=1, source_target_pairs={{0,24},{8,0},{16,8},{24,16},{1,25},{9,1},{17,9},{25,17},{2,26},{10... | collective-permute-start | bytes 294920 | tf_op jit(solution)/shard_map/ppermute | solution.py:23
  20.7 1.5 %collective-permute-start.2 = (bf16[48,1024]{1,0:T(8,128)(2,1)S(1)}, bf16[48,1024]{1,0:T(8,128)(2,1)S(1)}, u32[]{:S(2)}, u32[]{:S(2)}) collective-permute-start(bf16[48,1024]{1,0:T(8,128)(2,1)S(1)} %reshape.39), channel_id=1, source_target_pairs={{0,16},{8,24},{16,0},{24,8},{1,17},{9,25},{17,1},{25,9},{2,18},{10... | collective-permute-start | bytes 294920 | tf_op jit(solution)/shard_map/ppermute | solution.py:23
  22.3 0.7 broadcast_subtract_fusion
  23.0 0.2 reshape.41
  23.2 0.1 copy.5
  23.3 0.1 reshape.42
  23.6 2.4 %collective-permute-done.2 = bf16[48,1024]{1,0:T(8,128)(2,1)S(1)} collective-permute-done((bf16[48,1024]{1,0:T(8,128)(2,1)S(1)}, bf16[48,1024]{1,0:T(8,128)(2,1)S(1)}, u32[]{:S(2)}, u32[]{:S(2)}) %collective-permute-start.2) | collective-permute-done | bytes 98336 | tf_op jit(solution)/shard_map/ppermute | solution.py:23
  26.0 3.8 %collective-permute-start.3 = (bf16[192,1024]{1,0:T(8,128)(2,1)S(1)}, bf16[192,1024]{1,0:T(8,128)(2,1)S(1)}, u32[]{:S(2)}, u32[]{:S(2)}) collective-permute-start(bf16[192,1024]{1,0:T(8,128)(2,1)S(1)} %bitcast.20), channel_id=1, source_target_pairs={{0,1},{1,0},{2,3},{3,2},{4,5},{5,4},{6,7},{7,6},{8,9},{9,8},{10,11... | collective-permute-start | bytes 1179656 | tf_op jit(solution)/shard_map/ppermute | solution.py:23
  29.8 1.3 %collective-permute-start.4 = (bf16[192,1024]{1,0:T(8,128)(2,1)S(1)}, bf16[192,1024]{1,0:T(8,128)(2,1)S(1)}, u32[]{:S(2)}, u32[]{:S(2)}) collective-permute-start(bf16[192,1024]{1,0:T(8,128)(2,1)S(1)} %bitcast.21), channel_id=1, source_target_pairs={{0,2},{2,4},{4,6},{6,0},{1,3},{3,5},{5,7},{7,1},{8,10},{10,12},{12... | collective-permute-start | bytes 1179656 | tf_op jit(solution)/shard_map/ppermute | solution.py:23
  31.1 1.4 %collective-permute-start.6 = (bf16[192,1024]{1,0:T(8,128)(2,1)S(1)}, bf16[192,1024]{1,0:T(8,128)(2,1)S(1)}, u32[]{:S(2)}, u32[]{:S(2)}) collective-permute-start(bf16[192,1024]{1,0:T(8,128)(2,1)S(1)} %bitcast.22), channel_id=1, source_target_pairs={{0,6},{2,0},{4,2},{6,4},{1,7},{3,1},{5,3},{7,5},{8,14},{10,8},{12,... | collective-permute-start | bytes 1179656 | tf_op jit(solution)/shard_map/ppermute | solution.py:23
  32.6 9.2 %collective-permute-done.4.first = bf16[192,1024]{1,0:T(8,128)(2,1)S(1)} collective-permute-done((bf16[192,1024]{1,0:T(8,128)(2,1)S(1)}, bf16[192,1024]{1,0:T(8,128)(2,1)S(1)}, u32[]{:S(2)}, u32[]{:S(2)}) %collective-permute-start.4) | collective-permute-done | bytes 393248 | tf_op jit(solution)/shard_map/ppermute | solution.py:23
  41.8 0.9 %collective-permute-start.5 = (bf16[192,1024]{1,0:T(8,128)(2,1)S(1)}, bf16[192,1024]{1,0:T(8,128)(2,1)S(1)}, u32[]{:S(2)}, u32[]{:S(2)}) collective-permute-start(bf16[192,1024]{1,0:T(8,128)(2,1)S(1)} %collective-permute-done.4.first), channel_id=1, source_target_pairs={{0,1},{1,0},{2,3},{3,2},{4,5},{5,4},{6,7},{7,6},{8,9},{9,8},{10,11... | collective-permute-start | bytes 1179656 | tf_op jit(solution)/shard_map/ppermute | solution.py:23
  42.8 1.5 %collective-permute-start.8 = (bf16[192,1024]{1,0:T(8,128)(2,1)S(1)}, bf16[192,1024]{1,0:T(8,128)(2,1)S(1)}, u32[]{:S(2)}, u32[]{:S(2)}) collective-permute-start(bf16[192,1024]{1,0:T(8,128)(2,1)S(1)} %pick.1), channel_id=1, source_target_pairs={{0,2},{1,7},{2,4},{3,1},{4,6},{5,3},{6,0},{7,5},{8,10},{9,15},{10,... | collective-permute-start | bytes 1179656 | tf_op jit(solution)/shard_map/ppermute | solution.py:33
  44.4 2.9 %score.4 = f32[2,256]{1,0:T(2,128)S(1)} custom-call(bf16[256,1024]{1,0:T(8,128)(2,1)S(1)} %pad_maximum_fusion.3.queries, bf16[4096,1024]{1,0:T(8,128)(2,1)S(1)} %bitcast.19, s32[1,256]{1,0:T(1,128)S(1)} %prep.1.targets), custom_call_target="tpu_custom_call" | custom-call | flops 2147483648 | bytes 8912896 | tf_op jit(solution)/shard_map/score/pallas_call | solution.py:82
  47.4 0.1 broadcast_select_fusion.3
  47.6 2.8 %score.6 = f32[2,256]{1,0:T(2,128)S(1)} custom-call(bf16[256,1024]{1,0:T(8,128)(2,1)S(1)} %pad_maximum_fusion.2.queries, bf16[4096,1024]{1,0:T(8,128)(2,1)S(1)} %bitcast.19, s32[1,256]{1,0:T(1,128)S(1)} %get-tuple-element.43.targets), custom_call_target="tpu_custom_call" | custom-call | flops 2147483648 | bytes 8912896 | tf_op jit(solution)/shard_map/score/pallas_call | solution.py:82
  50.4 1.4 %collective-permute-start.9 = (bf16[192,1024]{1,0:T(8,128)(2,1)S(1)}, bf16[192,1024]{1,0:T(8,128)(2,1)S(1)}, u32[]{:S(2)}, u32[]{:S(2)}) collective-permute-start(bf16[192,1024]{1,0:T(8,128)(2,1)S(1)} %collective-permute-done.8), channel_id=1, source_target_pairs={{0,1},{1,0},{2,3},{3,2},{4,5},{5,4},{6,7},{7,6},{8,9},{9,8},{10,11... | collective-permute-start | bytes 1179656 | tf_op jit(solution)/shard_map/ppermute | solution.py:23
  51.9 5.1 %score.5 = f32[2,512]{1,0:T(2,128)S(1)} custom-call(bf16[512,1024]{1,0:T(8,128)(2,1)S(1)} %pad_maximum_fusion.queries, bf16[4096,1024]{1,0:T(8,128)(2,1)S(1)} %bitcast.19, s32[1,512]{1,0:T(1,128)S(1)} %get-tuple-element.42.targets), custom_call_target="tpu_custom_call" | custom-call | flops 4294967296 | bytes 9437184 | tf_op jit(solution)/shard_map/score/pallas_call | solution.py:82
  57.0 0.1 pad_maximum_fusion.1.queries
  57.1 5.1 %score.7 = f32[2,512]{1,0:T(2,128)S(1)} custom-call(bf16[512,1024]{1,0:T(8,128)(2,1)S(1)} %pad_maximum_fusion.1.queries, bf16[4096,1024]{1,0:T(8,128)(2,1)S(1)} %bitcast.19, s32[1,512]{1,0:T(1,128)S(1)} %get-tuple-element.45.targets), custom_call_target="tpu_custom_call" | custom-call | flops 4294967296 | bytes 9437184 | tf_op jit(solution)/shard_map/score/pallas_call | solution.py:82
  62.4 0.1 collective-permute-start.10
  62.5 1.1 %collective-permute-done.10 = f32[2,1536]{1,0:T(2,128)S(1)} collective-permute-done((f32[2,1536]{1,0:T(2,128)S(1)}, f32[2,1536]{1,0:T(2,128)S(1)}, u32[]{:S(2)}, u32[]{:S(2)}) %collective-permute-start.10) | collective-permute-done | bytes 12320 | tf_op jit(solution)/shard_map/ppermute | solution.py:23
  63.7 11.0 %all_to_all.16.parts = f32[16,2,1536]{2,1,0:T(2,128)S(1)} all-to-all(f32[16,2,1536]{2,1,0:T(2,128)S(1)} %join.2), channel_id=1, replica_groups=mesh['group'=8,'x'=4,'y'=4,'core'=2] {'x','y'}, dimensions={0} | all-to-all | bytes 393216 | tf_op jit(solution)/shard_map/all_to_all | solution.py:163
  74.7 0.1 join.3
  74.8 10.0 %all_to_all.17.parts = f32[8,2,1536]{2,1,0:T(2,128)S(1)} all-to-all(f32[8,2,1536]{2,1,0:T(2,128)S(1)} %join.3), channel_id=1, replica_groups=mesh['group'=8,'x'=4,'y'=4,'core'=2] {'group'}, dimensions={0} | all-to-all | bytes 196608 | tf_op jit(solution)/shard_map/all_to_all | solution.py:163
  84.9 0.7 close.1
  85.5 0.1 reshape.45
  85.7 0.1 copy.6
  85.8 0.8 reshape.46
  (46 shorter events, 0.9 us)
Async XLA Ops:
  18.0 5.6 %collective-permute-start = (bf16[48,1024]{1,0:T(8,128)(2,1)S(1)}, bf16[48,1024]{1,0:T(8,128)(2,1)S(1)}, u32[]{:S(2)}, u32[]{:S(2)}) collective-permute-start(bf16[48,1024]{1,0:T(8,128)(2,1)S(1)} %reshape.39), channel_id=1, source_target_pairs={{0,8},{8,16},{16,24},{24,0},{1,9},{9,17},{17,25},{25,1},{2,10},{10... | collective-permute-start | bytes 294920 | tf_op jit(solution)/shard_map/ppermute | solution.py:23
  19.3 4.3 %collective-permute-start.1 = (bf16[48,1024]{1,0:T(8,128)(2,1)S(1)}, bf16[48,1024]{1,0:T(8,128)(2,1)S(1)}, u32[]{:S(2)}, u32[]{:S(2)}) collective-permute-start(bf16[48,1024]{1,0:T(8,128)(2,1)S(1)} %reshape.39), channel_id=1, source_target_pairs={{0,24},{8,0},{16,8},{24,16},{1,25},{9,1},{17,9},{25,17},{2,26},{10... | collective-permute-start | bytes 294920 | tf_op jit(solution)/shard_map/ppermute | solution.py:23
  20.7 5.3 %collective-permute-start.2 = (bf16[48,1024]{1,0:T(8,128)(2,1)S(1)}, bf16[48,1024]{1,0:T(8,128)(2,1)S(1)}, u32[]{:S(2)}, u32[]{:S(2)}) collective-permute-start(bf16[48,1024]{1,0:T(8,128)(2,1)S(1)} %reshape.39), channel_id=1, source_target_pairs={{0,16},{8,24},{16,0},{24,8},{1,17},{9,25},{17,1},{25,9},{2,18},{10... | collective-permute-start | bytes 294920 | tf_op jit(solution)/shard_map/ppermute | solution.py:23
  26.0 18.4 %slice-start = ((s8[8388608]{0:T(1024)(128)(4,1)}), s8[4194304]{0:T(1024)(128)(4,1)S(1)}, s32[]{:S(2)}) async-start(s8[8388608]{0:T(1024)(128)(4,1)} %bitcast.18), calls=%async_computation.3 | async-start | bytes 8388608
  26.0 18.4 %slice-start.1 = ((s8[8388608]{0:T(1024)(128)(4,1)}), s8[4194304]{0:T(1024)(128)(4,1)S(1)}, s32[]{:S(2)}) async-start(s8[8388608]{0:T(1024)(128)(4,1)} %bitcast.18), calls=%async_computation.4 | async-start | bytes 8388608
  26.0 16.6 %collective-permute-start.3 = (bf16[192,1024]{1,0:T(8,128)(2,1)S(1)}, bf16[192,1024]{1,0:T(8,128)(2,1)S(1)}, u32[]{:S(2)}, u32[]{:S(2)}) collective-permute-start(bf16[192,1024]{1,0:T(8,128)(2,1)S(1)} %bitcast.20), channel_id=1, source_target_pairs={{0,1},{1,0},{2,3},{3,2},{4,5},{5,4},{6,7},{7,6},{8,9},{9,8},{10,11... | collective-permute-start | bytes 1179656 | tf_op jit(solution)/shard_map/ppermute | solution.py:23
  29.8 11.9 %collective-permute-start.4 = (bf16[192,1024]{1,0:T(8,128)(2,1)S(1)}, bf16[192,1024]{1,0:T(8,128)(2,1)S(1)}, u32[]{:S(2)}, u32[]{:S(2)}) collective-permute-start(bf16[192,1024]{1,0:T(8,128)(2,1)S(1)} %bitcast.21), channel_id=1, source_target_pairs={{0,2},{2,4},{4,6},{6,0},{1,3},{3,5},{5,7},{7,1},{8,10},{10,12},{12... | collective-permute-start | bytes 1179656 | tf_op jit(solution)/shard_map/ppermute | solution.py:23
  31.1 11.6 %collective-permute-start.6 = (bf16[192,1024]{1,0:T(8,128)(2,1)S(1)}, bf16[192,1024]{1,0:T(8,128)(2,1)S(1)}, u32[]{:S(2)}, u32[]{:S(2)}) collective-permute-start(bf16[192,1024]{1,0:T(8,128)(2,1)S(1)} %bitcast.22), channel_id=1, source_target_pairs={{0,6},{2,0},{4,2},{6,4},{1,7},{3,1},{5,3},{7,5},{8,14},{10,8},{12,... | collective-permute-start | bytes 1179656 | tf_op jit(solution)/shard_map/ppermute | solution.py:23
  41.8 5.5 %collective-permute-start.5 = (bf16[192,1024]{1,0:T(8,128)(2,1)S(1)}, bf16[192,1024]{1,0:T(8,128)(2,1)S(1)}, u32[]{:S(2)}, u32[]{:S(2)}) collective-permute-start(bf16[192,1024]{1,0:T(8,128)(2,1)S(1)} %collective-permute-done.4.first), channel_id=1, source_target_pairs={{0,1},{1,0},{2,3},{3,2},{4,5},{5,4},{6,7},{7,6},{8,9},{9,8},{10,11... | collective-permute-start | bytes 1179656 | tf_op jit(solution)/shard_map/ppermute | solution.py:23
  42.8 7.6 %collective-permute-start.8 = (bf16[192,1024]{1,0:T(8,128)(2,1)S(1)}, bf16[192,1024]{1,0:T(8,128)(2,1)S(1)}, u32[]{:S(2)}, u32[]{:S(2)}) collective-permute-start(bf16[192,1024]{1,0:T(8,128)(2,1)S(1)} %pick.1), channel_id=1, source_target_pairs={{0,2},{1,7},{2,4},{3,1},{4,6},{5,3},{6,0},{7,5},{8,10},{9,15},{10,... | collective-permute-start | bytes 1179656 | tf_op jit(solution)/shard_map/ppermute | solution.py:33
  44.3 3.0 %collective-permute-start.7 = (bf16[192,1024]{1,0:T(8,128)(2,1)S(1)}, bf16[192,1024]{1,0:T(8,128)(2,1)S(1)}, u32[]{:S(2)}, u32[]{:S(2)}) collective-permute-start(bf16[192,1024]{1,0:T(8,128)(2,1)S(1)} %collective-permute-done.6.second), channel_id=1, source_target_pairs={{0,1},{1,0},{2,3},{3,2},{4,5},{5,4},{6,7},{7,6},{8,9},{9,8},{10,11... | collective-permute-start | bytes 1179656 | tf_op jit(solution)/shard_map/ppermute | solution.py:23
  50.4 6.5 %collective-permute-start.9 = (bf16[192,1024]{1,0:T(8,128)(2,1)S(1)}, bf16[192,1024]{1,0:T(8,128)(2,1)S(1)}, u32[]{:S(2)}, u32[]{:S(2)}) collective-permute-start(bf16[192,1024]{1,0:T(8,128)(2,1)S(1)} %collective-permute-done.8), channel_id=1, source_target_pairs={{0,1},{1,0},{2,3},{3,2},{4,5},{5,4},{6,7},{7,6},{8,9},{9,8},{10,11... | collective-permute-start | bytes 1179656 | tf_op jit(solution)/shard_map/ppermute | solution.py:23
  62.4 1.3 %collective-permute-start.10 = (f32[2,1536]{1,0:T(2,128)S(1)}, f32[2,1536]{1,0:T(2,128)S(1)}, u32[]{:S(2)}, u32[]{:S(2)}) collective-permute-start(f32[2,1536]{1,0:T(2,128)S(1)} %bitcast.27), channel_id=1, source_target_pairs={{0,1},{1,0},{2,3},{3,2},{4,5},{5,4},{6,7},{7,6},{8,9},{9,8},{10,11... | collective-permute-start | bytes 36872 | tf_op jit(solution)/shard_map/ppermute | solution.py:23
